TPU v7x, 128 devices: a whole 4x4x4 slice. The times are simulated.
128 devices in a mesh: io: 16 (over z, y), cmp: 8 (over x, core).
Axes of the slice: x: 4, y: 4, z: 4, core: 2. Of those that a mesh axis runs over, the one named last changes fastest.
Arguments:
- fields: float32 [6, 8, 1024, 4096], P(None, None, 'cmp', 'io'), may hold values from -6 to 6
- mean_old: float32 [6, 8, 1024, 3072], P(None, 'cmp', 'io'), may hold values from -6 to 6
- land_mask: int32 [8, 1024, 4096], P('cmp', 'io'), may hold values from 0 to 1, as said below
Outputs:
- mean_new: float32 [6, 8, 1024, 3072], P(None, 'cmp', 'io')
- level_rms: float32 [6, 8], P(None, 'cmp')
Inputs may be any that keep to these rules, and one draw needn't show every extreme that they name: `land_mask`: each row (level, latitude) has between 1 and 3072 ocean points, and some row has exactly 3072.
All inputs are finite; a program needn't handle non-finite values.
Results may differ from a plain program's by a relative error of at most 0.00002.
Values sent between devices are 32-bit elements; how exact they have to be, the bound alone decides.
No kernel may reach another device: no remote copies, remote signals or barrier semaphores. Data moves between devices by JAX's collectives and lax.ppermute only.
A program may use at most 128 MiB of HBM per device.

v0:
```python
import jax
import jax.numpy as jnp
from jax import lax
from jax.experimental import pallas as pl
from jax.experimental.pallas import tpu as pltpu
from jax.sharding import PartitionSpec as P


STEPS = 3
LANES = 128
SUB = 8
ROUNDS = tuple(
    (kx, ks, kc) for kc in (0, 1) for pair in ((1, 3), (0, 2)) for ks in (1, 0) for kx in pair
)
STAGES = 5


def target_of(i, c, rnd):
    kx, ks, kc = rnd
    z, y, x = i >> 2, i & 3, c >> 1
    level = ((x - z + kx) & 3) * 2 + ((y >> 1) ^ kc)
    half = (y & 1) ^ ks
    return level, half


def source_block(b, l, rnd):
    kx, ks, kc = rnd
    z1, y1, x1, core1 = b >> 2, b & 3, l >> 1, l & 1
    z = (z1 - x1 + kx) & 3
    return z * 4 + (core1 ^ kc) * 2 + ((y1 & 1) ^ ks)


def pairs_of(rnd):
    out = []
    for i in range(16):
        for c in range(8):
            level, half = target_of(i, c, rnd)
            out.append((i * 8 + c, (2 * c + half) * 8 + level))
    return out


def cut_kernel(fields_ref, *refs):
    rounds = len(ROUNDS)
    outs, sem = refs[:rounds], refs[rounds]
    rows = outs[0].shape[1]
    i, c = lax.axis_index("io"), lax.axis_index("cmp")
    copies = []
    for r, rnd in enumerate(ROUNDS):
        level, half = target_of(i, c, rnd)
        band = pl.ds(pl.multiple_of(half * rows, rows), rows)
        copies.append(
            pltpu.make_async_copy(fields_ref.at[:, level, band, :], outs[r], sem.at[r])
        )
    for copy in copies:
        copy.start()
    for copy in copies:
        copy.wait()


def lane_gather(values, index):
    return jnp.take_along_axis(values, index, axis=1, mode="promise_in_bounds")


def index_kernel(mask_ref, lane_ref, move_ref, count_ref, dist_ref):
    rows, ncol = mask_ref.shape
    chunks = ncol // LANES
    before = lax.broadcasted_iota(jnp.int32, (LANES, LANES), 0) <= lax.broadcasted_iota(
        jnp.int32, (LANES, LANES), 1
    )
    upper = before.astype(jnp.bfloat16)
    ones = jnp.ones((LANES, LANES), jnp.bfloat16)
    lane = lax.broadcasted_iota(jnp.int32, (rows, LANES), 1)
    start = jnp.zeros((rows, LANES), jnp.int32)
    for k in range(chunks):
        cut = slice(k * LANES, (k + 1) * LANES)
        mask = mask_ref[:, cut]
        ocean = mask == 1
        mb = mask.astype(jnp.float32).astype(jnp.bfloat16)
        upto = jnp.dot(mb, upper, preferred_element_type=jnp.float32).astype(jnp.int32)
        total = jnp.dot(mb, ones, preferred_element_type=jnp.float32).astype(jnp.int32)
        state = jnp.where(ocean, ((lane - upto + 1) << 7) | lane, 0)
        for bit in range(7):
            moving = jnp.where((state >> (7 + bit)) & 1 == 1, state, 0)
            state = (state ^ moving) | pltpu.roll(moving, LANES - (1 << bit), 1)
        rank = (lane - start) & (LANES - 1)
        lane_ref[:, cut] = lane_gather(state & (LANES - 1), rank)
        chunk = (start + rank) >> 7
        dist_ref[:, cut] = jnp.where(rank < total, k - chunk, 0)
        start = start + total
    count_ref[...] = start
    for bit in range(STAGES):
        amount = 1 << bit
        for k in range(chunks):
            cut = slice(k * LANES, (k + 1) * LANES)
            here = dist_ref[:, cut]
            stay = jnp.where((here >> bit) & 1 == 1, 0, here)
            if k + amount < chunks:
                there = dist_ref[:, (k + amount) * LANES : (k + amount + 1) * LANES]
                arrive = there & amount
                move_ref[bit, :, cut] = arrive
                dist_ref[:, cut] = jnp.where(arrive != 0, there, stay)
            else:
                dist_ref[:, cut] = stay


def pack_kernel(lane_ref, move_ref, count_ref, old_ref, *refs):
    rounds = len(ROUNDS)
    pieces = refs[:rounds]
    new_ref, sum_ref, turned, out, acc, sem = refs[rounds:]
    fields, rows, width = old_ref.shape
    chunks = lane_ref.shape[1] // LANES
    groups = rows // SUB
    wide = width // LANES
    lane = lax.broadcasted_iota(jnp.int32, (SUB, LANES), 1)
    acc[...] = jnp.zeros_like(acc)
    io, cmp = lax.axis_index("io"), lax.axis_index("cmp")

    def copy_out(g, slot):
        return pltpu.make_async_copy(
            out.at[slot], new_ref.at[:, pl.ds(pl.multiple_of(g * SUB, SUB), SUB), :], sem.at[slot]
        )

    @pl.loop(0, groups)
    def _(g):
        slot = lax.rem(g, 2)
        band = pl.ds(pl.multiple_of(g * SUB, SUB), SUB)

        @pl.when(g >= 2)
        def _():
            copy_out(g - 2, slot).wait()

        left = count_ref[band, :] - lane
        for r in range(rounds):
            first = source_block(io, cmp, ROUNDS[r]) * 2
            for h in range(2):
                at = first + h
                index = lane_ref[band, pl.ds(pl.multiple_of(at * LANES, LANES), LANES)]
                for f in range(fields):
                    value = pieces[r][f, band, h * LANES : (h + 1) * LANES]
                    turned[f, at] = lane_gather(value, index)

        @pl.loop(0, fields)
        def _(f):
            values = [turned[f, k] for k in range(chunks)]
            for bit in range(STAGES):
                amount = 1 << bit
                for k in range(chunks - amount):
                    if bit == STAGES - 1 and k >= wide:
                        continue
                    arrive = move_ref[bit, band, k * LANES : (k + 1) * LANES] != 0
                    values[k] = jnp.where(arrive, values[k + amount], values[k])
            squares = acc[f]
            for k in range(wide):
                old = old_ref[f, band, k * LANES : (k + 1) * LANES]
                mean = (STEPS * old + values[k]) * (1.0 / (STEPS + 1.0))
                mean = jnp.where(left > k * LANES, mean, 0.0)
                out[slot, f, :, k * LANES : (k + 1) * LANES] = mean
                squares = squares + mean * mean
            acc[f] = squares

        copy_out(g, slot).start()

    row = lax.broadcasted_iota(jnp.int32, (SUB, LANES), 0)
    total = jnp.zeros((SUB, LANES), jnp.float32)
    for f in range(fields):
        total = jnp.where(row == f, jnp.sum(acc[f]), total)
    ocean = jnp.sum(jnp.where(lane[:1] == 0, count_ref[...], 0).astype(jnp.float32))
    total = jnp.where(row == fields, ocean, total)
    for p in range(sum_ref.shape[0]):
        sum_ref[p] = total
    for g in range(groups - 2, groups):
        copy_out(g, g % 2).wait()


VMEM = pl.BlockSpec(memory_space=pltpu.VMEM)


def cut(fields):
    nfield, _, nrow, ncol = fields.shape
    rounds = len(ROUNDS)
    piece = jax.ShapeDtypeStruct((nfield, nrow // 2, ncol), jnp.float32)
    return pl.pallas_call(
        cut_kernel,
        out_shape=(piece,) * rounds,
        in_specs=[pl.BlockSpec(memory_space=pltpu.HBM)],
        out_specs=(VMEM,) * rounds,
        scratch_shapes=[pltpu.SemaphoreType.DMA((rounds,))],
        compiler_params=pltpu.CompilerParams(vmem_limit_bytes=46 << 20),
        cost_estimate=pl.CostEstimate(flops=0, bytes_accessed=12 << 20, transcendentals=0),
        name="cut",
    )(fields)


def row_indices(mask):
    rows, ncol = mask.shape
    return pl.pallas_call(
        index_kernel,
        out_shape=(
            jax.ShapeDtypeStruct((rows, ncol), jnp.int32),
            jax.ShapeDtypeStruct((STAGES, rows, ncol), jnp.int32),
            jax.ShapeDtypeStruct((rows, LANES), jnp.int32),
        ),
        in_specs=[VMEM],
        out_specs=(VMEM, VMEM, VMEM),
        scratch_shapes=[pltpu.VMEM((rows, ncol), jnp.int32)],
        compiler_params=pltpu.CompilerParams(vmem_limit_bytes=3 << 20),
        cost_estimate=pl.CostEstimate(flops=20_000_000, bytes_accessed=12 << 20, transcendentals=0),
        name="row_indices",
    )(mask)


def pack(lanes, moves, counts, old, pieces, copies=16):
    fields, _, width = old.shape
    chunks = lanes.shape[1] // LANES
    return pl.pallas_call(
        pack_kernel,
        out_shape=(
            jax.ShapeDtypeStruct(old.shape, jnp.float32),
            jax.ShapeDtypeStruct((copies, SUB, LANES), jnp.float32),
        ),
        in_specs=[VMEM] * (4 + len(pieces)),
        out_specs=(pl.BlockSpec(memory_space=pltpu.HBM), VMEM),
        scratch_shapes=[
            pltpu.VMEM((fields, chunks, SUB, LANES), jnp.float32),
            pltpu.VMEM((2, fields, SUB, width), jnp.float32),
            pltpu.VMEM((fields, SUB, LANES), jnp.float32),
            pltpu.SemaphoreType.DMA((2,)),
        ],
        compiler_params=pltpu.CompilerParams(vmem_limit_bytes=12 << 20),
        cost_estimate=pl.CostEstimate(flops=40_000_000, bytes_accessed=16 << 20, transcendentals=0),
        name="pack",
    )(lanes, moves, counts, old, *pieces)


def on_device(fields, mean_old, land_mask):
    nfield = fields.shape[0]
    cuts = cut(fields)
    pieces = []
    for k, rnd in enumerate(ROUNDS):
        pieces.append(lax.ppermute(cuts[k], ("io", "cmp"), pairs_of(rnd)))
    lanes, moves, counts = row_indices(land_mask[0])
    mean_new, part = pack(lanes, moves, counts, mean_old[:, 0], pieces, lax.axis_size("io"))
    total = lax.all_to_all(part, "io", 0, 0, tiled=True)[:, : nfield + 1, :1].sum(axis=0)
    level_rms = jnp.sqrt(total[:nfield] / total[nfield] + 1e-06)
    return mean_new[:, None], level_rms


def solution(mesh):
    in_specs = (P(None, None, "cmp", "io"), P(None, "cmp", "io", None), P("cmp", "io", None))
    out_specs = (P(None, "cmp", "io", None), P(None, "cmp"))
    return jax.shard_map(
        on_device, mesh=mesh, in_specs=in_specs, out_specs=out_specs, check_vma=False
    )
```

profile of v0, /device:TPU:0, one launch (start us, length us, event | category | flops | bytes accessed | tf_op | source)
XLA Modules:
  0.0 134.3 jit_solution(14392331712330416251)
XLA Ops:
  0.6 3.1 %cut.1 = (f32[6,64,256]{2,1,0:T(8,128)S(1)}, f32[6,64,256]{2,1,0:T(8,128)S(1)}, f32[6,64,256]{2,1,0:T(8,128)S(1)}, f32[6,64,256]{2,1,0:T(8,128)S(1)}, f32[6,64,2...) custom-call(f32[6,8,128,256]{3,2,1,0:T(8,128)} %fields_ref.1), custom_call_target="tpu_custom_call" | custom-call | bytes 12582912 | tf_op jit(solution)/shard_map/cut/pallas_call | solution.py:182
  3.7 2.7 %collective-permute-start = (f32[6,64,256]{2,1,0:T(8,128)S(1)}, f32[6,64,256]{2,1,0:T(8,128)S(1)}, u32[]{:S(2)}, u32[]{:S(2)}) collective-permute-start(f32[6,64,256]{2,1,0:T(8,128)S(1)} %get-tuple-element.26), channel_id=1, source_target_pairs={{0,10},{1,26},{2,44},{3,60},{4,78},{5,94},{6,104},{7,120},{8,2},{9... | collective-permute-start | bytes 1179656 | tf_op jit(solution)/shard_map/ppermute | solution.py:240
  6.4 5.1 %collective-permute-start.1 = (f32[6,64,256]{2,1,0:T(8,128)S(1)}, f32[6,64,256]{2,1,0:T(8,128)S(1)}, u32[]{:S(2)}, u32[]{:S(2)}) collective-permute-start(f32[6,64,256]{2,1,0:T(8,128)S(1)} %get-tuple-element.27), channel_id=1, source_target_pairs={{0,14},{1,30},{2,40},{3,56},{4,74},{5,90},{6,108},{7,124},{8,6},{9... | collective-permute-start | bytes 1179656 | tf_op jit(solution)/shard_map/ppermute | solution.py:240
  11.5 1.9 %collective-permute-start.2 = (f32[6,64,256]{2,1,0:T(8,128)S(1)}, f32[6,64,256]{2,1,0:T(8,128)S(1)}, u32[]{:S(2)}, u32[]{:S(2)}) collective-permute-start(f32[6,64,256]{2,1,0:T(8,128)S(1)} %get-tuple-element.28), channel_id=1, source_target_pairs={{0,2},{1,18},{2,36},{3,52},{4,70},{5,86},{6,96},{7,112},{8,10},{9,... | collective-permute-start | bytes 1179656 | tf_op jit(solution)/shard_map/ppermute | solution.py:240
  13.4 3.7 %collective-permute-start.3 = (f32[6,64,256]{2,1,0:T(8,128)S(1)}, f32[6,64,256]{2,1,0:T(8,128)S(1)}, u32[]{:S(2)}, u32[]{:S(2)}) collective-permute-start(f32[6,64,256]{2,1,0:T(8,128)S(1)} %get-tuple-element.29), channel_id=1, source_target_pairs={{0,6},{1,22},{2,32},{3,48},{4,66},{5,82},{6,100},{7,116},{8,14},{9... | collective-permute-start | bytes 1179656 | tf_op jit(solution)/shard_map/ppermute | solution.py:240
  17.7 6.7 %collective-permute-start.5 = (f32[6,64,256]{2,1,0:T(8,128)S(1)}, f32[6,64,256]{2,1,0:T(8,128)S(1)}, u32[]{:S(2)}, u32[]{:S(2)}) collective-permute-start(f32[6,64,256]{2,1,0:T(8,128)S(1)} %get-tuple-element.31), channel_id=1, source_target_pairs={{0,12},{1,28},{2,46},{3,62},{4,72},{5,88},{6,106},{7,122},{8,4},{9... | collective-permute-start | bytes 1179656 | tf_op jit(solution)/shard_map/ppermute | solution.py:240
  24.4 0.7 collective-permute-start.6
  25.1 8.3 %collective-permute-start.7 = (f32[6,64,256]{2,1,0:T(8,128)S(1)}, f32[6,64,256]{2,1,0:T(8,128)S(1)}, u32[]{:S(2)}, u32[]{:S(2)}) collective-permute-start(f32[6,64,256]{2,1,0:T(8,128)S(1)} %get-tuple-element.33), channel_id=1, source_target_pairs={{0,4},{1,20},{2,38},{3,54},{4,64},{5,80},{6,98},{7,114},{8,12},{9,... | collective-permute-start | bytes 1179656 | tf_op jit(solution)/shard_map/ppermute | solution.py:240
  33.4 8.3 %collective-permute-done.3.refs_3_ = f32[6,64,256]{2,1,0:T(8,128)S(1)} collective-permute-done((f32[6,64,256]{2,1,0:T(8,128)S(1)}, f32[6,64,256]{2,1,0:T(8,128)S(1)}, u32[]{:S(2)}, u32[]{:S(2)}) %collective-permute-start.3) | collective-permute-done | bytes 393248 | tf_op jit(solution)/shard_map/ppermute | solution.py:240
  41.7 2.9 %collective-permute-start.8 = (f32[6,64,256]{2,1,0:T(8,128)S(1)}, f32[6,64,256]{2,1,0:T(8,128)S(1)}, u32[]{:S(2)}, u32[]{:S(2)}) collective-permute-start(f32[6,64,256]{2,1,0:T(8,128)S(1)} %get-tuple-element.34), channel_id=1, source_target_pairs={{0,11},{1,27},{2,45},{3,61},{4,79},{5,95},{6,105},{7,121},{8,3},{9... | collective-permute-start | bytes 1179656 | tf_op jit(solution)/shard_map/ppermute | solution.py:240
  44.6 3.0 %collective-permute-start.9 = (f32[6,64,256]{2,1,0:T(8,128)S(1)}, f32[6,64,256]{2,1,0:T(8,128)S(1)}, u32[]{:S(2)}, u32[]{:S(2)}) collective-permute-start(f32[6,64,256]{2,1,0:T(8,128)S(1)} %get-tuple-element.35), channel_id=1, source_target_pairs={{0,15},{1,31},{2,41},{3,57},{4,75},{5,91},{6,109},{7,125},{8,7},{9... | collective-permute-start | bytes 1179656 | tf_op jit(solution)/shard_map/ppermute | solution.py:240
  47.6 3.7 %collective-permute-start.10 = (f32[6,64,256]{2,1,0:T(8,128)S(1)}, f32[6,64,256]{2,1,0:T(8,128)S(1)}, u32[]{:S(2)}, u32[]{:S(2)}) collective-permute-start(f32[6,64,256]{2,1,0:T(8,128)S(1)} %get-tuple-element.36), channel_id=1, source_target_pairs={{0,3},{1,19},{2,37},{3,53},{4,71},{5,87},{6,97},{7,113},{8,11},{9,... | collective-permute-start | bytes 1179656 | tf_op jit(solution)/shard_map/ppermute | solution.py:240
  51.3 7.4 %collective-permute-start.11 = (f32[6,64,256]{2,1,0:T(8,128)S(1)}, f32[6,64,256]{2,1,0:T(8,128)S(1)}, u32[]{:S(2)}, u32[]{:S(2)}) collective-permute-start(f32[6,64,256]{2,1,0:T(8,128)S(1)} %get-tuple-element.37), channel_id=1, source_target_pairs={{0,7},{1,23},{2,33},{3,49},{4,67},{5,83},{6,101},{7,117},{8,15},{9... | collective-permute-start | bytes 1179656 | tf_op jit(solution)/shard_map/ppermute | solution.py:240
  58.8 1.5 %collective-permute-start.12 = (f32[6,64,256]{2,1,0:T(8,128)S(1)}, f32[6,64,256]{2,1,0:T(8,128)S(1)}, u32[]{:S(2)}, u32[]{:S(2)}) collective-permute-start(f32[6,64,256]{2,1,0:T(8,128)S(1)} %get-tuple-element.38), channel_id=1, source_target_pairs={{0,9},{1,25},{2,43},{3,59},{4,77},{5,93},{6,111},{7,127},{8,1},{9,... | collective-permute-start | bytes 1179656 | tf_op jit(solution)/shard_map/ppermute | solution.py:240
  60.2 5.8 %collective-permute-start.13 = (f32[6,64,256]{2,1,0:T(8,128)S(1)}, f32[6,64,256]{2,1,0:T(8,128)S(1)}, u32[]{:S(2)}, u32[]{:S(2)}) collective-permute-start(f32[6,64,256]{2,1,0:T(8,128)S(1)} %get-tuple-element.39), channel_id=1, source_target_pairs={{0,13},{1,29},{2,47},{3,63},{4,73},{5,89},{6,107},{7,123},{8,5},{9... | collective-permute-start | bytes 1179656 | tf_op jit(solution)/shard_map/ppermute | solution.py:240
  66.0 0.6 collective-permute-done.9.refs_9_
  66.6 5.6 %collective-permute-start.14 = (f32[6,64,256]{2,1,0:T(8,128)S(1)}, f32[6,64,256]{2,1,0:T(8,128)S(1)}, u32[]{:S(2)}, u32[]{:S(2)}) collective-permute-start(f32[6,64,256]{2,1,0:T(8,128)S(1)} %get-tuple-element.40), channel_id=1, source_target_pairs={{0,1},{1,17},{2,35},{3,51},{4,69},{5,85},{6,103},{7,119},{8,9},{9,... | collective-permute-start | bytes 1179656 | tf_op jit(solution)/shard_map/ppermute | solution.py:240
  72.3 1.2 collective-permute-start.15
  73.5 11.5 %row_indices.1 = (s32[64,4096]{1,0:T(8,128)S(1)}, s32[5,64,4096]{2,1,0:T(8,128)S(1)}, s32[64,128]{1,0:T(8,128)S(1)}) custom-call(s32[64,4096]{1,0:T(8,128)S(1)} %bitcast.9), custom_call_target="tpu_custom_call" | custom-call | flops 20000000 | bytes 12582912 | tf_op jit(solution)/shard_map/row_indices/pallas_call | solution.py:196
  85.0 12.5 %collective-permute-done.13.refs_13_ = f32[6,64,256]{2,1,0:T(8,128)S(1)} collective-permute-done((f32[6,64,256]{2,1,0:T(8,128)S(1)}, f32[6,64,256]{2,1,0:T(8,128)S(1)}, u32[]{:S(2)}, u32[]{:S(2)}) %collective-permute-start.13) | collective-permute-done | bytes 393248 | tf_op jit(solution)/shard_map/ppermute | solution.py:240
  97.6 7.8 %pack.1 = (f32[6,64,3072]{2,1,0:T(8,128)}, f32[16,8,128]{2,1,0:T(8,128)S(1)}) custom-call(s32[64,4096]{1,0:T(8,128)S(1)} %get-tuple-element.23.lane_ref, s32[5,64,4096]{2,1,0:T(8,128)S(1)} %get-tuple-element.24.move_ref, s32[64,128]{1,0:T(8,128)S(1)} %get-tuple-element.25.count_ref, f32[6,64,3072]{2,1,0:T(8,128)S(1)} %bitcast.8, ...), custom_call_target="tpu_custom_call" | custom-call | flops 40000000 | bytes 16777216 | tf_op jit(solution)/shard_map/pack/pallas_call | solution.py:215
  105.3 27.0 %all_to_all.5 = f32[16,8,128]{2,1,0:T(8,128)S(1)} all-to-all(f32[16,8,128]{2,1,0:T(8,128)S(1)} %get-tuple-element.43), channel_id=1, replica_groups=mesh['io'=16,'cmp'=8] {'io'}, dimensions={0} | all-to-all | bytes 131072 | tf_op jit(solution)/shard_map/all_to_all | solution.py:243
  132.4 0.7 slice.13
  133.1 1.2 sqrt_bitcast_fusion
  (19 shorter events, 0.7 us)
Async XLA Ops:
  0.6 72.9 %copy-start.1 = (s32[1,64,4096]{2,1,0:T(8,128)S(1)}, s32[1,64,4096]{2,1,0:T(8,128)}, u32[]{:S(2)}) copy-start(s32[1,64,4096]{2,1,0:T(8,128)} %param.5) | copy-start | bytes 3145732
  0.6 96.9 %copy-start = (f32[6,1,64,3072]{3,2,1,0:T(8,128)S(1)}, f32[6,1,64,3072]{3,2,1,0:T(8,128)}, u32[]{:S(2)}) copy-start(f32[6,1,64,3072]{3,2,1,0:T(8,128)} %param.4) | copy-start | bytes 14155780
  3.7 14.0 %collective-permute-start = (f32[6,64,256]{2,1,0:T(8,128)S(1)}, f32[6,64,256]{2,1,0:T(8,128)S(1)}, u32[]{:S(2)}, u32[]{:S(2)}) collective-permute-start(f32[6,64,256]{2,1,0:T(8,128)S(1)} %get-tuple-element.26), channel_id=1, source_target_pairs={{0,10},{1,26},{2,44},{3,60},{4,78},{5,94},{6,104},{7,120},{8,2},{9... | collective-permute-start | bytes 1179656 | tf_op jit(solution)/shard_map/ppermute | solution.py:240
  6.4 18.0 %collective-permute-start.1 = (f32[6,64,256]{2,1,0:T(8,128)S(1)}, f32[6,64,256]{2,1,0:T(8,128)S(1)}, u32[]{:S(2)}, u32[]{:S(2)}) collective-permute-start(f32[6,64,256]{2,1,0:T(8,128)S(1)} %get-tuple-element.27), channel_id=1, source_target_pairs={{0,14},{1,30},{2,40},{3,56},{4,74},{5,90},{6,108},{7,124},{8,6},{9... | collective-permute-start | bytes 1179656 | tf_op jit(solution)/shard_map/ppermute | solution.py:240
  11.5 13.6 %collective-permute-start.2 = (f32[6,64,256]{2,1,0:T(8,128)S(1)}, f32[6,64,256]{2,1,0:T(8,128)S(1)}, u32[]{:S(2)}, u32[]{:S(2)}) collective-permute-start(f32[6,64,256]{2,1,0:T(8,128)S(1)} %get-tuple-element.28), channel_id=1, source_target_pairs={{0,2},{1,18},{2,36},{3,52},{4,70},{5,86},{6,96},{7,112},{8,10},{9,... | collective-permute-start | bytes 1179656 | tf_op jit(solution)/shard_map/ppermute | solution.py:240
  13.4 28.3 %collective-permute-start.3 = (f32[6,64,256]{2,1,0:T(8,128)S(1)}, f32[6,64,256]{2,1,0:T(8,128)S(1)}, u32[]{:S(2)}, u32[]{:S(2)}) collective-permute-start(f32[6,64,256]{2,1,0:T(8,128)S(1)} %get-tuple-element.29), channel_id=1, source_target_pairs={{0,6},{1,22},{2,32},{3,48},{4,66},{5,82},{6,100},{7,116},{8,14},{9... | collective-permute-start | bytes 1179656 | tf_op jit(solution)/shard_map/ppermute | solution.py:240
  17.1 27.5 %collective-permute-start.4 = (f32[6,64,256]{2,1,0:T(8,128)S(1)}, f32[6,64,256]{2,1,0:T(8,128)S(1)}, u32[]{:S(2)}, u32[]{:S(2)}) collective-permute-start(f32[6,64,256]{2,1,0:T(8,128)S(1)} %get-tuple-element.30), channel_id=1, source_target_pairs={{0,8},{1,24},{2,42},{3,58},{4,76},{5,92},{6,110},{7,126},{8,0},{9,... | collective-permute-start | bytes 1179656 | tf_op jit(solution)/shard_map/ppermute | solution.py:240
  17.7 29.9 %collective-permute-start.5 = (f32[6,64,256]{2,1,0:T(8,128)S(1)}, f32[6,64,256]{2,1,0:T(8,128)S(1)}, u32[]{:S(2)}, u32[]{:S(2)}) collective-permute-start(f32[6,64,256]{2,1,0:T(8,128)S(1)} %get-tuple-element.31), channel_id=1, source_target_pairs={{0,12},{1,28},{2,46},{3,62},{4,72},{5,88},{6,106},{7,122},{8,4},{9... | collective-permute-start | bytes 1179656 | tf_op jit(solution)/shard_map/ppermute | solution.py:240
  24.4 26.9 %collective-permute-start.6 = (f32[6,64,256]{2,1,0:T(8,128)S(1)}, f32[6,64,256]{2,1,0:T(8,128)S(1)}, u32[]{:S(2)}, u32[]{:S(2)}) collective-permute-start(f32[6,64,256]{2,1,0:T(8,128)S(1)} %get-tuple-element.32), channel_id=1, source_target_pairs={{0,0},{1,16},{2,34},{3,50},{4,68},{5,84},{6,102},{7,118},{8,8},{9,... | collective-permute-start | bytes 1179656 | tf_op jit(solution)/shard_map/ppermute | solution.py:240
  25.1 33.7 %collective-permute-start.7 = (f32[6,64,256]{2,1,0:T(8,128)S(1)}, f32[6,64,256]{2,1,0:T(8,128)S(1)}, u32[]{:S(2)}, u32[]{:S(2)}) collective-permute-start(f32[6,64,256]{2,1,0:T(8,128)S(1)} %get-tuple-element.33), channel_id=1, source_target_pairs={{0,4},{1,20},{2,38},{3,54},{4,64},{5,80},{6,98},{7,114},{8,12},{9,... | collective-permute-start | bytes 1179656 | tf_op jit(solution)/shard_map/ppermute | solution.py:240
  41.7 18.5 %collective-permute-start.8 = (f32[6,64,256]{2,1,0:T(8,128)S(1)}, f32[6,64,256]{2,1,0:T(8,128)S(1)}, u32[]{:S(2)}, u32[]{:S(2)}) collective-permute-start(f32[6,64,256]{2,1,0:T(8,128)S(1)} %get-tuple-element.34), channel_id=1, source_target_pairs={{0,11},{1,27},{2,45},{3,61},{4,79},{5,95},{6,105},{7,121},{8,3},{9... | collective-permute-start | bytes 1179656 | tf_op jit(solution)/shard_map/ppermute | solution.py:240
  44.6 22.0 %collective-permute-start.9 = (f32[6,64,256]{2,1,0:T(8,128)S(1)}, f32[6,64,256]{2,1,0:T(8,128)S(1)}, u32[]{:S(2)}, u32[]{:S(2)}) collective-permute-start(f32[6,64,256]{2,1,0:T(8,128)S(1)} %get-tuple-element.35), channel_id=1, source_target_pairs={{0,15},{1,31},{2,41},{3,57},{4,75},{5,91},{6,109},{7,125},{8,7},{9... | collective-permute-start | bytes 1179656 | tf_op jit(solution)/shard_map/ppermute | solution.py:240
  47.6 24.6 %collective-permute-start.10 = (f32[6,64,256]{2,1,0:T(8,128)S(1)}, f32[6,64,256]{2,1,0:T(8,128)S(1)}, u32[]{:S(2)}, u32[]{:S(2)}) collective-permute-start(f32[6,64,256]{2,1,0:T(8,128)S(1)} %get-tuple-element.36), channel_id=1, source_target_pairs={{0,3},{1,19},{2,37},{3,53},{4,71},{5,87},{6,97},{7,113},{8,11},{9,... | collective-permute-start | bytes 1179656 | tf_op jit(solution)/shard_map/ppermute | solution.py:240
  51.3 33.7 %collective-permute-start.11 = (f32[6,64,256]{2,1,0:T(8,128)S(1)}, f32[6,64,256]{2,1,0:T(8,128)S(1)}, u32[]{:S(2)}, u32[]{:S(2)}) collective-permute-start(f32[6,64,256]{2,1,0:T(8,128)S(1)} %get-tuple-element.37), channel_id=1, source_target_pairs={{0,7},{1,23},{2,33},{3,49},{4,67},{5,83},{6,101},{7,117},{8,15},{9... | collective-permute-start | bytes 1179656 | tf_op jit(solution)/shard_map/ppermute | solution.py:240
  58.8 26.3 %collective-permute-start.12 = (f32[6,64,256]{2,1,0:T(8,128)S(1)}, f32[6,64,256]{2,1,0:T(8,128)S(1)}, u32[]{:S(2)}, u32[]{:S(2)}) collective-permute-start(f32[6,64,256]{2,1,0:T(8,128)S(1)} %get-tuple-element.38), channel_id=1, source_target_pairs={{0,9},{1,25},{2,43},{3,59},{4,77},{5,93},{6,111},{7,127},{8,1},{9,... | collective-permute-start | bytes 1179656 | tf_op jit(solution)/shard_map/ppermute | solution.py:240
  60.2 37.3 %collective-permute-start.13 = (f32[6,64,256]{2,1,0:T(8,128)S(1)}, f32[6,64,256]{2,1,0:T(8,128)S(1)}, u32[]{:S(2)}, u32[]{:S(2)}) collective-permute-start(f32[6,64,256]{2,1,0:T(8,128)S(1)} %get-tuple-element.39), channel_id=1, source_target_pairs={{0,13},{1,29},{2,47},{3,63},{4,73},{5,89},{6,107},{7,123},{8,5},{9... | collective-permute-start | bytes 1179656 | tf_op jit(solution)/shard_map/ppermute | solution.py:240
  66.6 30.9 %collective-permute-start.14 = (f32[6,64,256]{2,1,0:T(8,128)S(1)}, f32[6,64,256]{2,1,0:T(8,128)S(1)}, u32[]{:S(2)}, u32[]{:S(2)}) collective-permute-start(f32[6,64,256]{2,1,0:T(8,128)S(1)} %get-tuple-element.40), channel_id=1, source_target_pairs={{0,1},{1,17},{2,35},{3,51},{4,69},{5,85},{6,103},{7,119},{8,9},{9,... | collective-permute-start | bytes 1179656 | tf_op jit(solution)/shard_map/ppermute | solution.py:240
  72.3 25.3 %collective-permute-start.15 = (f32[6,64,256]{2,1,0:T(8,128)S(1)}, f32[6,64,256]{2,1,0:T(8,128)S(1)}, u32[]{:S(2)}, u32[]{:S(2)}) collective-permute-start(f32[6,64,256]{2,1,0:T(8,128)S(1)} %get-tuple-element.41), channel_id=1, source_target_pairs={{0,5},{1,21},{2,39},{3,55},{4,65},{5,81},{6,99},{7,115},{8,13},{9,... | collective-permute-start | bytes 1179656 | tf_op jit(solution)/shard_map/ppermute | solution.py:240
where the time goes:
time: 135 us; the launch traced here: 134 us
  starting transfers between devices  60.8 us (45%)
  blocking collectives  27 us (20%)
  Pallas kernels  22.4 us (17%)
  waiting for transfers between devices  21.5 us (16%)
    ppermute x16, starting transfers between devices, on_device(): pieces.append(lax.ppermute(cuts[k], ('io', 'cmp'), pairs_of(rnd)))  60.8 us
    all_to_all x1, blocking collectives, on_device(): lax.all_to_all(part, 'io', 0, 0, tiled=True)[:, :nfield + 1, :1].sum(axis=0)  27 us
    ppermute x16, waiting for transfers between devices, on_device(): pieces.append(lax.ppermute(cuts[k], ('io', 'cmp'), pairs_of(rnd)))  21.5 us
    pallas_call x1, Pallas kernels, row_indices(): pl.pallas_call(index_kernel, out_shape=(jax.ShapeDtypeStruct((rows, ncol)...  11.5 us
    pallas_call x1, Pallas kernels, pack(): pl.pallas_call(pack_kernel, out_shape=(jax.ShapeDtypeStruct(old.shape, jn...  7.78 us
    pallas_call x1, Pallas kernels, cut(): pl.pallas_call(cut_kernel, out_shape=(piece,) * rounds, in_specs=[pl.Bloc...  3.07 us
  transfers between devices with their start and end apart: 16, of which 3 were waited for; matrix products, arithmetic and copies ran while one was open for 0% of the time, Pallas kernels for 9%

commit v1 on v0

--- a/solution.py
+++ b/solution.py
@@ -1,3 +1,5 @@
+import functools
+
 import jax
 import jax.numpy as jnp
 from jax import lax
@@ -10,9 +12,11 @@
 LANES = 128
 SUB = 8
 ROUNDS = tuple(
-    (kx, ks, kc) for kc in (0, 1) for pair in ((1, 3), (0, 2)) for ks in (1, 0) for kx in pair
+    (kx, ks, kc) for pair in ((1, 3), (0, 2)) for ks in (1, 0) for kc in (0, 1) for kx in pair
 )
 STAGES = 5
+TURNS = (0, 8, 13, 16)
+SHARE = 3
 
 
 def target_of(i, c, rnd):
@@ -61,7 +65,7 @@
     return jnp.take_along_axis(values, index, axis=1, mode="promise_in_bounds")
 
 
-def index_kernel(mask_ref, lane_ref, move_ref, count_ref, dist_ref):
+def index_kernel(mask_ref, old_ref, lane_ref, move_ref, count_ref, share_ref, dist_ref):
     rows, ncol = mask_ref.shape
     chunks = ncol // LANES
     before = lax.broadcasted_iota(jnp.int32, (LANES, LANES), 0) <= lax.broadcasted_iota(
@@ -88,6 +92,8 @@
         dist_ref[:, cut] = jnp.where(rank < total, k - chunk, 0)
         start = start + total
     count_ref[...] = start
+    for f in range(old_ref.shape[0]):
+        share_ref[f] = old_ref[f] * (STEPS / (STEPS + 1.0))
     for bit in range(STAGES):
         amount = 1 << bit
         for k in range(chunks):
@@ -103,73 +109,111 @@
                 dist_ref[:, cut] = stay
 
 
-def pack_kernel(lane_ref, move_ref, count_ref, old_ref, *refs):
-    rounds = len(ROUNDS)
-    pieces = refs[:rounds]
-    new_ref, sum_ref, turned, out, acc, sem = refs[rounds:]
-    fields, rows, width = old_ref.shape
-    chunks = lane_ref.shape[1] // LANES
-    groups = rows // SUB
-    wide = width // LANES
-    lane = lax.broadcasted_iota(jnp.int32, (SUB, LANES), 1)
-    acc[...] = jnp.zeros_like(acc)
+def turn_kernel(rounds, reuse, lane_ref, *refs):
+    pieces = refs[: len(rounds)]
+    turned = refs[len(rounds) + reuse]
+    fields, rows, _ = pieces[0].shape
     io, cmp = lax.axis_index("io"), lax.axis_index("cmp")
 
-    def copy_out(g, slot):
-        return pltpu.make_async_copy(
-            out.at[slot], new_ref.at[:, pl.ds(pl.multiple_of(g * SUB, SUB), SUB), :], sem.at[slot]
-        )
-
-    @pl.loop(0, groups)
+    @pl.loop(0, rows // SUB)
     def _(g):
-        slot = lax.rem(g, 2)
         band = pl.ds(pl.multiple_of(g * SUB, SUB), SUB)
-
-        @pl.when(g >= 2)
-        def _():
-            copy_out(g - 2, slot).wait()
-
-        left = count_ref[band, :] - lane
-        for r in range(rounds):
-            first = source_block(io, cmp, ROUNDS[r]) * 2
+        for r, rnd in enumerate(rounds):
+            first = source_block(io, cmp, rnd) * 2
             for h in range(2):
                 at = first + h
                 index = lane_ref[band, pl.ds(pl.multiple_of(at * LANES, LANES), LANES)]
                 for f in range(fields):
                     value = pieces[r][f, band, h * LANES : (h + 1) * LANES]
-                    turned[f, at] = lane_gather(value, index)
-
-        @pl.loop(0, fields)
-        def _(f):
-            values = [turned[f, k] for k in range(chunks)]
-            for bit in range(STAGES):
-                amount = 1 << bit
-                for k in range(chunks - amount):
-                    if bit == STAGES - 1 and k >= wide:
-                        continue
-                    arrive = move_ref[bit, band, k * LANES : (k + 1) * LANES] != 0
-                    values[k] = jnp.where(arrive, values[k + amount], values[k])
-            squares = acc[f]
-            for k in range(wide):
-                old = old_ref[f, band, k * LANES : (k + 1) * LANES]
-                mean = (STEPS * old + values[k]) * (1.0 / (STEPS + 1.0))
-                mean = jnp.where(left > k * LANES, mean, 0.0)
-                out[slot, f, :, k * LANES : (k + 1) * LANES] = mean
-                squares = squares + mean * mean
-            acc[f] = squares
+                    turned[f, at, band, :] = lane_gather(value, index) * (1.0 / (STEPS + 1.0))
+
+
+def moved_chunks(turned, move_ref, fs, band, wide):
+    chunks = turned.shape[1]
+    level = [{} for _ in range(STAGES + 1)]
+
+    def settle(bit, k):
+        if bit == STAGES:
+            return
+        amount = 1 << bit
+        for at in (k - amount, k):
+            if at < 0 or at in level[bit + 1] or (at + amount < chunks and at == k):
+                continue
+            value = level[bit].pop(at)
+            if at + amount < chunks:
+                arrive = move_ref[bit, band, at * LANES : (at + 1) * LANES] != 0
+                near = level[bit][at + amount]
+                value = [jnp.where(arrive, n, v) for n, v in zip(near, value)]
+            level[bit + 1][at] = value
+            settle(bit + 1, at)
+
+    done = 0
+    for k in range(chunks):
+        level[0][k] = [turned[f, k, band, :] for f in fs]
+        settle(0, k)
+        while done < wide and done in level[STAGES]:
+            yield done, level[STAGES].pop(done)
+            level[STAGES][done] = None
+            done += 1
+
+
+def pack_kernel(turned, move_ref, count_ref, old_ref, new_ref, sum_ref, out, acc, sem):
+    fields, rows, width = old_ref.shape
+    groups = rows // SUB
+    wide = width // LANES
+    lane = lax.broadcasted_iota(jnp.int32, (SUB, LANES), 1)
+    acc[...] = jnp.zeros_like(acc)
+
+    def copy_out(g, slot):
+        return pltpu.make_async_copy(
+            out.at[slot], new_ref.at[:, pl.ds(pl.multiple_of(g * SUB, SUB), SUB), :], sem.at[slot]
+        )
+
+    @pl.loop(0, groups)
+    def _(g):
+        slot = lax.rem(g, 2)
+        band = pl.ds(pl.multiple_of(g * SUB, SUB), SUB)
+
+        @pl.when(g >= 2)
+        def _():
+            copy_out(g - 2, slot).wait()
+
+        left = count_ref[band, :] - lane
+
+        @pl.loop(0, fields, step=SHARE)
+        def _(f0):
+            fs = [f0 + j for j in range(SHARE)]
+            squares = [acc[f] for f in fs]
+            for k, values in moved_chunks(turned, move_ref, fs, band, wide):
+                valid = left > k * LANES
+                cut = slice(k * LANES, (k + 1) * LANES)
+                for j, f in enumerate(fs):
+                    mean = jnp.where(valid, old_ref[f, band, cut] + values[j], 0.0)
+                    out[slot, f, :, cut] = mean
+                    squares[j] = squares[j] + mean * mean
+            for j, f in enumerate(fs):
+                acc[f] = squares[j]
 
         copy_out(g, slot).start()
 
     row = lax.broadcasted_iota(jnp.int32, (SUB, LANES), 0)
     total = jnp.zeros((SUB, LANES), jnp.float32)
     for f in range(fields):
-        total = jnp.where(row == f, jnp.sum(acc[f]), total)
+        total = jnp.where(lane == f, jnp.sum(acc[f]), total)
     ocean = jnp.sum(jnp.where(lane[:1] == 0, count_ref[...], 0).astype(jnp.float32))
-    total = jnp.where(row == fields, ocean, total)
+    total = jnp.where(row == 1, ocean, total)
     for p in range(sum_ref.shape[0]):
         sum_ref[p] = total
     for g in range(groups - 2, groups):
         copy_out(g, g % 2).wait()
+
+
+def finish_kernel(part_ref, rms_ref):
+    total = part_ref[0]
+    for p in range(1, part_ref.shape[0]):
+        total = total + part_ref[p]
+    rms = jnp.sqrt(total[0:1] / total[1:2] + 1e-06)
+    rms_ref[...] = rms[:, : rms_ref.shape[1]]
 
 
 VMEM = pl.BlockSpec(memory_space=pltpu.VMEM)
@@ -191,7 +235,7 @@
     )(fields)
 
 
-def row_indices(mask):
+def row_indices(mask, old):
     rows, ncol = mask.shape
     return pl.pallas_call(
         index_kernel,
@@ -199,37 +243,65 @@
             jax.ShapeDtypeStruct((rows, ncol), jnp.int32),
             jax.ShapeDtypeStruct((STAGES, rows, ncol), jnp.int32),
             jax.ShapeDtypeStruct((rows, LANES), jnp.int32),
+            jax.ShapeDtypeStruct(old.shape, jnp.float32),
         ),
-        in_specs=[VMEM],
-        out_specs=(VMEM, VMEM, VMEM),
+        in_specs=[VMEM, VMEM],
+        out_specs=(VMEM,) * 4,
         scratch_shapes=[pltpu.VMEM((rows, ncol), jnp.int32)],
         compiler_params=pltpu.CompilerParams(vmem_limit_bytes=3 << 20),
         cost_estimate=pl.CostEstimate(flops=20_000_000, bytes_accessed=12 << 20, transcendentals=0),
         name="row_indices",
-    )(mask)
-
-
-def pack(lanes, moves, counts, old, pieces, copies=16):
+    )(mask, old)
+
+
+def turn(rounds, lanes, pieces, turned):
+    fields, rows, _ = pieces[0].shape
+    shape = jax.ShapeDtypeStruct((fields, lanes.shape[1] // LANES, rows, LANES), jnp.float32)
+    before = [] if turned is None else [turned]
+    return pl.pallas_call(
+        functools.partial(turn_kernel, rounds, len(before)),
+        out_shape=shape,
+        in_specs=[VMEM] * (1 + len(pieces) + len(before)),
+        out_specs=VMEM,
+        input_output_aliases={1 + len(pieces): 0} if before else {},
+        compiler_params=pltpu.CompilerParams(vmem_limit_bytes=2 << 20),
+        cost_estimate=pl.CostEstimate(
+            flops=1_000_000 * len(pieces), bytes_accessed=800_000 * len(pieces), transcendentals=0
+        ),
+        name="turn",
+    )(lanes, *pieces, *before)
+
+
+def pack(turned, moves, counts, old, copies=16):
     fields, _, width = old.shape
-    chunks = lanes.shape[1] // LANES
     return pl.pallas_call(
         pack_kernel,
         out_shape=(
             jax.ShapeDtypeStruct(old.shape, jnp.float32),
             jax.ShapeDtypeStruct((copies, SUB, LANES), jnp.float32),
         ),
-        in_specs=[VMEM] * (4 + len(pieces)),
+        in_specs=[VMEM] * 4,
         out_specs=(pl.BlockSpec(memory_space=pltpu.HBM), VMEM),
         scratch_shapes=[
-            pltpu.VMEM((fields, chunks, SUB, LANES), jnp.float32),
             pltpu.VMEM((2, fields, SUB, width), jnp.float32),
             pltpu.VMEM((fields, SUB, LANES), jnp.float32),
             pltpu.SemaphoreType.DMA((2,)),
         ],
-        compiler_params=pltpu.CompilerParams(vmem_limit_bytes=12 << 20),
+        compiler_params=pltpu.CompilerParams(vmem_limit_bytes=6 << 20),
         cost_estimate=pl.CostEstimate(flops=40_000_000, bytes_accessed=16 << 20, transcendentals=0),
         name="pack",
-    )(lanes, moves, counts, old, *pieces)
+    )(turned, moves, counts, old)
+
+
+def finish(part, fields):
+    return pl.pallas_call(
+        finish_kernel,
+        out_shape=jax.ShapeDtypeStruct((1, fields), jnp.float32),
+        in_specs=[VMEM],
+        out_specs=VMEM,
+        compiler_params=pltpu.CompilerParams(vmem_limit_bytes=1 << 20),
+        name="finish",
+    )(part)
 
 
 def on_device(fields, mean_old, land_mask):
@@ -238,11 +310,13 @@
     pieces = []
     for k, rnd in enumerate(ROUNDS):
         pieces.append(lax.ppermute(cuts[k], ("io", "cmp"), pairs_of(rnd)))
-    lanes, moves, counts = row_indices(land_mask[0])
-    mean_new, part = pack(lanes, moves, counts, mean_old[:, 0], pieces, lax.axis_size("io"))
-    total = lax.all_to_all(part, "io", 0, 0, tiled=True)[:, : nfield + 1, :1].sum(axis=0)
-    level_rms = jnp.sqrt(total[:nfield] / total[nfield] + 1e-06)
-    return mean_new[:, None], level_rms
+    lanes, moves, counts, share = row_indices(land_mask[0], mean_old[:, 0])
+    turned = None
+    for low, high in zip(TURNS, TURNS[1:]):
+        turned = turn(ROUNDS[low:high], lanes, pieces[low:high], turned)
+    mean_new, part = pack(turned, moves, counts, share, lax.axis_size("io"))
+    rms = finish(lax.all_to_all(part, "io", 0, 0, tiled=True), nfield)
+    return mean_new[:, None], rms.T
 
 
 def solution(mesh):

time: 135 us -> 147 us (1.089)
  starting transfers between devices: 60.8 us -> 86.3 us
  waiting for transfers between devices: 21.5 us -> 6.83 us
  Pallas kernels: 22.4 us -> 24.6 us
  blocking collectives: 27 us -> 28.5 us
    ppermute x16, starting transfers between devices: 60.8 us -> 86.3 us  [on_device(): pieces.append(lax.ppermute(cuts[k], ('io', 'cmp'), pairs_of(rnd)))]
    ppermute x16, waiting for transfers between devices: 21.5 us -> 6.83 us  [on_device(): pieces.append(lax.ppermute(cuts[k], ('io', 'cmp'), pairs_of(rnd)))]
    pallas_call x0 -> x4, Pallas kernels: none -> 4.64 us  [the longest x3 4.1 us: turn(): pl.pallas_call(functools.partial(turn_kernel, rounds, len(before)), out_s...]
    pallas_call x1, Pallas kernels: 7.78 us -> 5.13 us  [pack(): pl.pallas_call(pack_kernel, out_shape=(jax.ShapeDtypeStruct(old.shape, jn...]
    all_to_all x1, blocking collectives: 27 us -> 28.5 us  [on_device(): rms = finish(lax.all_to_all(part, 'io', 0, 0, tiled=True), nfield)]
  transfers between devices with their start and end apart: 16 -> 16, of which waited for: 3 -> 2; matrix products, arithmetic and copies ran while one was open for 0% -> 0% of each run, Pallas kernels for 9% -> 10%
where the time goes in v1:
time: 147 us
  starting transfers between devices  86.3 us (59%)
  blocking collectives  28.5 us (19%)
  Pallas kernels  24.6 us (17%)
  waiting for transfers between devices  6.83 us (5%)
    ppermute x16, starting transfers between devices, on_device(): pieces.append(lax.ppermute(cuts[k], ('io', 'cmp'), pairs_of(rnd)))  86.3 us
    all_to_all x1, blocking collectives, on_device(): rms = finish(lax.all_to_all(part, 'io', 0, 0, tiled=True), nfield)  28.5 us
    pallas_call x1, Pallas kernels, row_indices(): pl.pallas_call(index_kernel, out_shape=(jax.ShapeDtypeStruct((rows, ncol)...  11.7 us
    ppermute x16, waiting for transfers between devices, on_device(): pieces.append(lax.ppermute(cuts[k], ('io', 'cmp'), pairs_of(rnd)))  6.83 us
    pallas_call x1, Pallas kernels, pack(): pl.pallas_call(pack_kernel, out_shape=(jax.ShapeDtypeStruct(old.shape, jn...  5.13 us
    pallas_call x3, Pallas kernels, turn(): pl.pallas_call(functools.partial(turn_kernel, rounds, len(before)), out_s...  4.1 us
    pallas_call x1, Pallas kernels, cut(): pl.pallas_call(cut_kernel, out_shape=(piece,) * rounds, in_specs=[pl.Bloc...  3.07 us
  transfers between devices with their start and end apart: 16, of which 2 were waited for; matrix products, arithmetic and copies ran while one was open for 0% of the time, Pallas kernels for 10%

profile of v1, /device:TPU:0, one launch (start us, length us, event | category | flops | bytes accessed | tf_op | source)
XLA Modules:
  0.0 146.9 jit_solution(11943035905890546177)
XLA Ops:
  0.6 3.1 %cut.1 = (f32[6,64,256]{2,1,0:T(8,128)S(1)}, f32[6,64,256]{2,1,0:T(8,128)S(1)}, f32[6,64,256]{2,1,0:T(8,128)S(1)}, f32[6,64,256]{2,1,0:T(8,128)S(1)}, f32[6,64,2...) custom-call(f32[6,8,128,256]{3,2,1,0:T(8,128)} %fields_ref.1), custom_call_target="tpu_custom_call" | custom-call | bytes 12582912 | tf_op jit(solution)/shard_map/cut/pallas_call | solution.py:226
  3.7 1.8 %collective-permute-start.3 = (f32[6,64,256]{2,1,0:T(8,128)S(1)}, f32[6,64,256]{2,1,0:T(8,128)S(1)}, u32[]{:S(2)}, u32[]{:S(2)}) collective-permute-start(f32[6,64,256]{2,1,0:T(8,128)S(1)} %get-tuple-element.28), channel_id=1, source_target_pairs={{0,8},{1,24},{2,42},{3,58},{4,76},{5,92},{6,110},{7,126},{8,0},{9,... | collective-permute-start | bytes 1179656 | tf_op jit(solution)/shard_map/ppermute | solution.py:312
  5.5 6.2 %collective-permute-start.4 = (f32[6,64,256]{2,1,0:T(8,128)S(1)}, f32[6,64,256]{2,1,0:T(8,128)S(1)}, u32[]{:S(2)}, u32[]{:S(2)}) collective-permute-start(f32[6,64,256]{2,1,0:T(8,128)S(1)} %get-tuple-element.29), channel_id=1, source_target_pairs={{0,12},{1,28},{2,46},{3,62},{4,72},{5,88},{6,106},{7,122},{8,4},{9... | collective-permute-start | bytes 1179656 | tf_op jit(solution)/shard_map/ppermute | solution.py:312
  11.7 0.7 collective-permute-start.5
  12.4 1.6 %collective-permute-start.8 = (f32[6,64,256]{2,1,0:T(8,128)S(1)}, f32[6,64,256]{2,1,0:T(8,128)S(1)}, u32[]{:S(2)}, u32[]{:S(2)}) collective-permute-start(f32[6,64,256]{2,1,0:T(8,128)S(1)} %get-tuple-element.33), channel_id=1, source_target_pairs={{0,10},{1,26},{2,44},{3,60},{4,78},{5,94},{6,104},{7,120},{8,2},{9... | collective-permute-start | bytes 1179656 | tf_op jit(solution)/shard_map/ppermute | solution.py:312
  14.0 5.4 %collective-permute-start.9 = (f32[6,64,256]{2,1,0:T(8,128)S(1)}, f32[6,64,256]{2,1,0:T(8,128)S(1)}, u32[]{:S(2)}, u32[]{:S(2)}) collective-permute-start(f32[6,64,256]{2,1,0:T(8,128)S(1)} %get-tuple-element.34), channel_id=1, source_target_pairs={{0,14},{1,30},{2,40},{3,56},{4,74},{5,90},{6,108},{7,124},{8,6},{9... | collective-permute-start | bytes 1179656 | tf_op jit(solution)/shard_map/ppermute | solution.py:312
  19.4 1.7 %collective-permute-start.10 = (f32[6,64,256]{2,1,0:T(8,128)S(1)}, f32[6,64,256]{2,1,0:T(8,128)S(1)}, u32[]{:S(2)}, u32[]{:S(2)}) collective-permute-start(f32[6,64,256]{2,1,0:T(8,128)S(1)} %get-tuple-element.35), channel_id=1, source_target_pairs={{0,11},{1,27},{2,45},{3,61},{4,79},{5,95},{6,105},{7,121},{8,3},{9... | collective-permute-start | bytes 1179656 | tf_op jit(solution)/shard_map/ppermute | solution.py:312
  21.2 30.6 %collective-permute-start.11 = (f32[6,64,256]{2,1,0:T(8,128)S(1)}, f32[6,64,256]{2,1,0:T(8,128)S(1)}, u32[]{:S(2)}, u32[]{:S(2)}) collective-permute-start(f32[6,64,256]{2,1,0:T(8,128)S(1)} %get-tuple-element.36), channel_id=1, source_target_pairs={{0,15},{1,31},{2,41},{3,57},{4,75},{5,91},{6,109},{7,125},{8,7},{9... | collective-permute-start | bytes 1179656 | tf_op jit(solution)/shard_map/ppermute | solution.py:312
  51.8 1.9 %collective-permute-start.12 = (f32[6,64,256]{2,1,0:T(8,128)S(1)}, f32[6,64,256]{2,1,0:T(8,128)S(1)}, u32[]{:S(2)}, u32[]{:S(2)}) collective-permute-start(f32[6,64,256]{2,1,0:T(8,128)S(1)} %get-tuple-element.37), channel_id=1, source_target_pairs={{0,2},{1,18},{2,36},{3,52},{4,70},{5,86},{6,96},{7,112},{8,10},{9,... | collective-permute-start | bytes 1179656 | tf_op jit(solution)/shard_map/ppermute | solution.py:312
  53.7 1.9 %collective-permute-start.13 = (f32[6,64,256]{2,1,0:T(8,128)S(1)}, f32[6,64,256]{2,1,0:T(8,128)S(1)}, u32[]{:S(2)}, u32[]{:S(2)}) collective-permute-start(f32[6,64,256]{2,1,0:T(8,128)S(1)} %get-tuple-element.38), channel_id=1, source_target_pairs={{0,6},{1,22},{2,32},{3,48},{4,66},{5,82},{6,100},{7,116},{8,14},{9... | collective-permute-start | bytes 1179656 | tf_op jit(solution)/shard_map/ppermute | solution.py:312
  55.7 5.2 %collective-permute-start.14 = (f32[6,64,256]{2,1,0:T(8,128)S(1)}, f32[6,64,256]{2,1,0:T(8,128)S(1)}, u32[]{:S(2)}, u32[]{:S(2)}) collective-permute-start(f32[6,64,256]{2,1,0:T(8,128)S(1)} %get-tuple-element.39), channel_id=1, source_target_pairs={{0,3},{1,19},{2,37},{3,53},{4,71},{5,87},{6,97},{7,113},{8,11},{9,... | collective-permute-start | bytes 1179656 | tf_op jit(solution)/shard_map/ppermute | solution.py:312
  60.9 3.1 %collective-permute-start.15 = (f32[6,64,256]{2,1,0:T(8,128)S(1)}, f32[6,64,256]{2,1,0:T(8,128)S(1)}, u32[]{:S(2)}, u32[]{:S(2)}) collective-permute-start(f32[6,64,256]{2,1,0:T(8,128)S(1)} %get-tuple-element.40), channel_id=1, source_target_pairs={{0,7},{1,23},{2,33},{3,49},{4,67},{5,83},{6,101},{7,117},{8,15},{9... | collective-permute-start | bytes 1179656 | tf_op jit(solution)/shard_map/ppermute | solution.py:312
  64.0 3.7 %collective-permute-start.6 = (f32[6,64,256]{2,1,0:T(8,128)S(1)}, f32[6,64,256]{2,1,0:T(8,128)S(1)}, u32[]{:S(2)}, u32[]{:S(2)}) collective-permute-start(f32[6,64,256]{2,1,0:T(8,128)S(1)} %get-tuple-element.31), channel_id=1, source_target_pairs={{0,13},{1,29},{2,47},{3,63},{4,73},{5,89},{6,107},{7,123},{8,5},{9... | collective-permute-start | bytes 1179656 | tf_op jit(solution)/shard_map/ppermute | solution.py:312
  67.7 1.5 %collective-permute-done.12.refs_4_ = f32[6,64,256]{2,1,0:T(8,128)S(1)} collective-permute-done((f32[6,64,256]{2,1,0:T(8,128)S(1)}, f32[6,64,256]{2,1,0:T(8,128)S(1)}, u32[]{:S(2)}, u32[]{:S(2)}) %collective-permute-start.12) | collective-permute-done | bytes 393248 | tf_op jit(solution)/shard_map/ppermute | solution.py:312
  69.2 0.7 collective-permute-start.7
  69.9 5.0 %collective-permute-start = (f32[6,64,256]{2,1,0:T(8,128)S(1)}, f32[6,64,256]{2,1,0:T(8,128)S(1)}, u32[]{:S(2)}, u32[]{:S(2)}) collective-permute-start(f32[6,64,256]{2,1,0:T(8,128)S(1)} %get-tuple-element.25), channel_id=1, source_target_pairs={{0,4},{1,20},{2,38},{3,54},{4,64},{5,80},{6,98},{7,114},{8,12},{9,... | collective-permute-start | bytes 1179656 | tf_op jit(solution)/shard_map/ppermute | solution.py:312
  74.9 16.7 %collective-permute-start.1 = (f32[6,64,256]{2,1,0:T(8,128)S(1)}, f32[6,64,256]{2,1,0:T(8,128)S(1)}, u32[]{:S(2)}, u32[]{:S(2)}) collective-permute-start(f32[6,64,256]{2,1,0:T(8,128)S(1)} %get-tuple-element.26), channel_id=1, source_target_pairs={{0,1},{1,17},{2,35},{3,51},{4,69},{5,85},{6,103},{7,119},{8,9},{9,... | collective-permute-start | bytes 1179656 | tf_op jit(solution)/shard_map/ppermute | solution.py:312
  91.6 5.2 %collective-permute-done.15.refs_7_ = f32[6,64,256]{2,1,0:T(8,128)S(1)} collective-permute-done((f32[6,64,256]{2,1,0:T(8,128)S(1)}, f32[6,64,256]{2,1,0:T(8,128)S(1)}, u32[]{:S(2)}, u32[]{:S(2)}) %collective-permute-start.15) | collective-permute-done | bytes 393248 | tf_op jit(solution)/shard_map/ppermute | solution.py:312
  96.9 11.7 %row_indices.1 = (s32[64,4096]{1,0:T(8,128)S(1)}, s32[5,64,4096]{2,1,0:T(8,128)S(1)}, s32[64,128]{1,0:T(8,128)S(1)}, f32[6,64,3072]{2,1,0:T(8,128)S(1)}) custom-call(s32[64,4096]{1,0:T(8,128)S(1)} %bitcast.7, f32[6,64,3072]{2,1,0:T(8,128)S(1)} %bitcast.6), custom_call_target="tpu_custom_call" | custom-call | flops 20000000 | bytes 12582912 | tf_op jit(solution)/shard_map/row_indices/pallas_call | solution.py:240
  108.6 1.8 %turn.3.refs_5_ = f32[6,32,64,128]{3,2,1,0:T(8,128)S(1)} custom-call(s32[64,4096]{1,0:T(8,128)S(1)} %get-tuple-element.24.lane_ref, f32[6,64,256]{2,1,0:T(8,128)S(1)} %collective-permute-done.8.refs_0_, f32[6,64,256]{2,1,0:T(8,128)S(1)} %collective-permute-done.9.refs_1_, f32[6,64,256]{2,1,0:T(8,128)S(1)} %collective-permute-done.10.refs_2_, ...), custom_call_target="tpu_custom_call" | custom-call | flops 8000000 | bytes 6400000 | tf_op jit(solution)/shard_map/turn/pallas_call | solution.py:261
  110.4 1.3 turn.4.refs_3_
  111.8 1.0 turn.5.turned
  112.8 5.1 %pack.1 = (f32[6,64,3072]{2,1,0:T(8,128)}, f32[16,8,128]{2,1,0:T(8,128)S(1)}) custom-call(f32[6,32,64,128]{3,2,1,0:T(8,128)S(1)} %turn.5.turned, s32[5,64,4096]{2,1,0:T(8,128)S(1)} %get-tuple-element.41.move_ref, s32[64,128]{1,0:T(8,128)S(1)} %get-tuple-element.42.count_ref, f32[6,64,3072]{2,1,0:T(8,128)S(1)} %get-tuple-element.43.old_ref), custom_call_target="tpu_custom_call" | custom-call | flops 40000000 | bytes 16777216 | tf_op jit(solution)/shard_map/pack/pallas_call | solution.py:277
  117.9 28.5 %all_to_all.5.part_ref = f32[16,8,128]{2,1,0:T(8,128)S(1)} all-to-all(f32[16,8,128]{2,1,0:T(8,128)S(1)} %get-tuple-element.45), channel_id=1, replica_groups=mesh['io'=16,'cmp'=8] {'io'}, dimensions={0} | all-to-all | bytes 131072 | tf_op jit(solution)/shard_map/all_to_all | solution.py:318
  (20 shorter events, 0.6 us)
Async XLA Ops:
  0.6 96.3 %copy-start.1 = (s32[1,64,4096]{2,1,0:T(8,128)S(1)}, s32[1,64,4096]{2,1,0:T(8,128)}, u32[]{:S(2)}) copy-start(s32[1,64,4096]{2,1,0:T(8,128)} %param.5) | copy-start | bytes 3145732
  0.6 96.2 %copy-start = (f32[6,1,64,3072]{3,2,1,0:T(8,128)S(1)}, f32[6,1,64,3072]{3,2,1,0:T(8,128)}, u32[]{:S(2)}) copy-start(f32[6,1,64,3072]{3,2,1,0:T(8,128)} %param.4) | copy-start | bytes 14155780
  3.7 15.7 %collective-permute-start.3 = (f32[6,64,256]{2,1,0:T(8,128)S(1)}, f32[6,64,256]{2,1,0:T(8,128)S(1)}, u32[]{:S(2)}, u32[]{:S(2)}) collective-permute-start(f32[6,64,256]{2,1,0:T(8,128)S(1)} %get-tuple-element.28), channel_id=1, source_target_pairs={{0,8},{1,24},{2,42},{3,58},{4,76},{5,92},{6,110},{7,126},{8,0},{9,... | collective-permute-start | bytes 1179656 | tf_op jit(solution)/shard_map/ppermute | solution.py:312
  5.5 15.7 %collective-permute-start.4 = (f32[6,64,256]{2,1,0:T(8,128)S(1)}, f32[6,64,256]{2,1,0:T(8,128)S(1)}, u32[]{:S(2)}, u32[]{:S(2)}) collective-permute-start(f32[6,64,256]{2,1,0:T(8,128)S(1)} %get-tuple-element.29), channel_id=1, source_target_pairs={{0,12},{1,28},{2,46},{3,62},{4,72},{5,88},{6,106},{7,122},{8,4},{9... | collective-permute-start | bytes 1179656 | tf_op jit(solution)/shard_map/ppermute | solution.py:312
  11.7 40.1 %collective-permute-start.5 = (f32[6,64,256]{2,1,0:T(8,128)S(1)}, f32[6,64,256]{2,1,0:T(8,128)S(1)}, u32[]{:S(2)}, u32[]{:S(2)}) collective-permute-start(f32[6,64,256]{2,1,0:T(8,128)S(1)} %get-tuple-element.30), channel_id=1, source_target_pairs={{0,9},{1,25},{2,43},{3,59},{4,77},{5,93},{6,111},{7,127},{8,1},{9,... | collective-permute-start | bytes 1179656 | tf_op jit(solution)/shard_map/ppermute | solution.py:312
  12.4 41.3 %collective-permute-start.8 = (f32[6,64,256]{2,1,0:T(8,128)S(1)}, f32[6,64,256]{2,1,0:T(8,128)S(1)}, u32[]{:S(2)}, u32[]{:S(2)}) collective-permute-start(f32[6,64,256]{2,1,0:T(8,128)S(1)} %get-tuple-element.33), channel_id=1, source_target_pairs={{0,10},{1,26},{2,44},{3,60},{4,78},{5,94},{6,104},{7,120},{8,2},{9... | collective-permute-start | bytes 1179656 | tf_op jit(solution)/shard_map/ppermute | solution.py:312
  14.0 41.6 %collective-permute-start.9 = (f32[6,64,256]{2,1,0:T(8,128)S(1)}, f32[6,64,256]{2,1,0:T(8,128)S(1)}, u32[]{:S(2)}, u32[]{:S(2)}) collective-permute-start(f32[6,64,256]{2,1,0:T(8,128)S(1)} %get-tuple-element.34), channel_id=1, source_target_pairs={{0,14},{1,30},{2,40},{3,56},{4,74},{5,90},{6,108},{7,124},{8,6},{9... | collective-permute-start | bytes 1179656 | tf_op jit(solution)/shard_map/ppermute | solution.py:312
  19.4 41.4 %collective-permute-start.10 = (f32[6,64,256]{2,1,0:T(8,128)S(1)}, f32[6,64,256]{2,1,0:T(8,128)S(1)}, u32[]{:S(2)}, u32[]{:S(2)}) collective-permute-start(f32[6,64,256]{2,1,0:T(8,128)S(1)} %get-tuple-element.35), channel_id=1, source_target_pairs={{0,11},{1,27},{2,45},{3,61},{4,79},{5,95},{6,105},{7,121},{8,3},{9... | collective-permute-start | bytes 1179656 | tf_op jit(solution)/shard_map/ppermute | solution.py:312
  21.2 42.8 %collective-permute-start.11 = (f32[6,64,256]{2,1,0:T(8,128)S(1)}, f32[6,64,256]{2,1,0:T(8,128)S(1)}, u32[]{:S(2)}, u32[]{:S(2)}) collective-permute-start(f32[6,64,256]{2,1,0:T(8,128)S(1)} %get-tuple-element.36), channel_id=1, source_target_pairs={{0,15},{1,31},{2,41},{3,57},{4,75},{5,91},{6,109},{7,125},{8,7},{9... | collective-permute-start | bytes 1179656 | tf_op jit(solution)/shard_map/ppermute | solution.py:312
  51.8 17.4 %collective-permute-start.12 = (f32[6,64,256]{2,1,0:T(8,128)S(1)}, f32[6,64,256]{2,1,0:T(8,128)S(1)}, u32[]{:S(2)}, u32[]{:S(2)}) collective-permute-start(f32[6,64,256]{2,1,0:T(8,128)S(1)} %get-tuple-element.37), channel_id=1, source_target_pairs={{0,2},{1,18},{2,36},{3,52},{4,70},{5,86},{6,96},{7,112},{8,10},{9,... | collective-permute-start | bytes 1179656 | tf_op jit(solution)/shard_map/ppermute | solution.py:312
  53.7 16.2 %collective-permute-start.13 = (f32[6,64,256]{2,1,0:T(8,128)S(1)}, f32[6,64,256]{2,1,0:T(8,128)S(1)}, u32[]{:S(2)}, u32[]{:S(2)}) collective-permute-start(f32[6,64,256]{2,1,0:T(8,128)S(1)} %get-tuple-element.38), channel_id=1, source_target_pairs={{0,6},{1,22},{2,32},{3,48},{4,66},{5,82},{6,100},{7,116},{8,14},{9... | collective-permute-start | bytes 1179656 | tf_op jit(solution)/shard_map/ppermute | solution.py:312
  55.7 19.3 %collective-permute-start.14 = (f32[6,64,256]{2,1,0:T(8,128)S(1)}, f32[6,64,256]{2,1,0:T(8,128)S(1)}, u32[]{:S(2)}, u32[]{:S(2)}) collective-permute-start(f32[6,64,256]{2,1,0:T(8,128)S(1)} %get-tuple-element.39), channel_id=1, source_target_pairs={{0,3},{1,19},{2,37},{3,53},{4,71},{5,87},{6,97},{7,113},{8,11},{9,... | collective-permute-start | bytes 1179656 | tf_op jit(solution)/shard_map/ppermute | solution.py:312
  60.9 36.0 %collective-permute-start.15 = (f32[6,64,256]{2,1,0:T(8,128)S(1)}, f32[6,64,256]{2,1,0:T(8,128)S(1)}, u32[]{:S(2)}, u32[]{:S(2)}) collective-permute-start(f32[6,64,256]{2,1,0:T(8,128)S(1)} %get-tuple-element.40), channel_id=1, source_target_pairs={{0,7},{1,23},{2,33},{3,49},{4,67},{5,83},{6,101},{7,117},{8,15},{9... | collective-permute-start | bytes 1179656 | tf_op jit(solution)/shard_map/ppermute | solution.py:312
  64.0 46.4 %collective-permute-start.6 = (f32[6,64,256]{2,1,0:T(8,128)S(1)}, f32[6,64,256]{2,1,0:T(8,128)S(1)}, u32[]{:S(2)}, u32[]{:S(2)}) collective-permute-start(f32[6,64,256]{2,1,0:T(8,128)S(1)} %get-tuple-element.31), channel_id=1, source_target_pairs={{0,13},{1,29},{2,47},{3,63},{4,73},{5,89},{6,107},{7,123},{8,5},{9... | collective-permute-start | bytes 1179656 | tf_op jit(solution)/shard_map/ppermute | solution.py:312
  69.2 41.2 %collective-permute-start.7 = (f32[6,64,256]{2,1,0:T(8,128)S(1)}, f32[6,64,256]{2,1,0:T(8,128)S(1)}, u32[]{:S(2)}, u32[]{:S(2)}) collective-permute-start(f32[6,64,256]{2,1,0:T(8,128)S(1)} %get-tuple-element.32), channel_id=1, source_target_pairs={{0,0},{1,16},{2,34},{3,50},{4,68},{5,84},{6,102},{7,118},{8,8},{9,... | collective-permute-start | bytes 1179656 | tf_op jit(solution)/shard_map/ppermute | solution.py:312
  69.9 41.8 %collective-permute-start = (f32[6,64,256]{2,1,0:T(8,128)S(1)}, f32[6,64,256]{2,1,0:T(8,128)S(1)}, u32[]{:S(2)}, u32[]{:S(2)}) collective-permute-start(f32[6,64,256]{2,1,0:T(8,128)S(1)} %get-tuple-element.25), channel_id=1, source_target_pairs={{0,4},{1,20},{2,38},{3,54},{4,64},{5,80},{6,98},{7,114},{8,12},{9,... | collective-permute-start | bytes 1179656 | tf_op jit(solution)/shard_map/ppermute | solution.py:312
  74.9 36.8 %collective-permute-start.1 = (f32[6,64,256]{2,1,0:T(8,128)S(1)}, f32[6,64,256]{2,1,0:T(8,128)S(1)}, u32[]{:S(2)}, u32[]{:S(2)}) collective-permute-start(f32[6,64,256]{2,1,0:T(8,128)S(1)} %get-tuple-element.26), channel_id=1, source_target_pairs={{0,1},{1,17},{2,35},{3,51},{4,69},{5,85},{6,103},{7,119},{8,9},{9,... | collective-permute-start | bytes 1179656 | tf_op jit(solution)/shard_map/ppermute | solution.py:312
  96.9 14.9 %collective-permute-start.2 = (f32[6,64,256]{2,1,0:T(8,128)S(1)}, f32[6,64,256]{2,1,0:T(8,128)S(1)}, u32[]{:S(2)}, u32[]{:S(2)}) collective-permute-start(f32[6,64,256]{2,1,0:T(8,128)S(1)} %get-tuple-element.27), channel_id=1, source_target_pairs={{0,5},{1,21},{2,39},{3,55},{4,65},{5,81},{6,99},{7,115},{8,13},{9,... | collective-permute-start | bytes 1179656 | tf_op jit(solution)/shard_map/ppermute | solution.py:312

commit v2 on v1

--- a/solution.py
+++ b/solution.py
@@ -12,11 +12,17 @@
 LANES = 128
 SUB = 8
 ROUNDS = tuple(
-    (kx, ks, kc) for pair in ((1, 3), (0, 2)) for ks in (1, 0) for kc in (0, 1) for kx in pair
+    (pair[j ^ kc], ks, kc)
+    for pair in ((1, 3), (0, 2))
+    for ks in (1, 0)
+    for kc in (0, 1)
+    for j in (0, 1)
 )
 STAGES = 5
-TURNS = (0, 8, 13, 16)
-SHARE = 3
+TURNS = (0, 8, 13, 15, 16)
+CUTS = (0, 4, 16)
+GRANTS = (204, 192)
+SHARE = 2
 
 
 def target_of(i, c, rnd):
@@ -43,13 +49,12 @@
     return out
 
 
-def cut_kernel(fields_ref, *refs):
-    rounds = len(ROUNDS)
-    outs, sem = refs[:rounds], refs[rounds]
+def cut_kernel(rounds, fields_ref, *refs):
+    outs, sem = refs[: len(rounds)], refs[len(rounds)]
     rows = outs[0].shape[1]
     i, c = lax.axis_index("io"), lax.axis_index("cmp")
     copies = []
-    for r, rnd in enumerate(ROUNDS):
+    for r, rnd in enumerate(rounds):
         level, half = target_of(i, c, rnd)
         band = pl.ds(pl.multiple_of(half * rows, rows), rows)
         copies.append(
@@ -164,9 +169,10 @@
     lane = lax.broadcasted_iota(jnp.int32, (SUB, LANES), 1)
     acc[...] = jnp.zeros_like(acc)
 
-    def copy_out(g, slot):
+    def copy_out(g, slot, f0):
+        fs, band = pl.ds(f0, SHARE), pl.ds(pl.multiple_of(g * SUB, SUB), SUB)
         return pltpu.make_async_copy(
-            out.at[slot], new_ref.at[:, pl.ds(pl.multiple_of(g * SUB, SUB), SUB), :], sem.at[slot]
+            out.at[slot, fs], new_ref.at[fs, band, :], sem.at[slot, f0 // SHARE]
         )
 
     @pl.loop(0, groups)
@@ -174,15 +180,16 @@
         slot = lax.rem(g, 2)
         band = pl.ds(pl.multiple_of(g * SUB, SUB), SUB)
 
-        @pl.when(g >= 2)
-        def _():
-            copy_out(g - 2, slot).wait()
-
         left = count_ref[band, :] - lane
 
         @pl.loop(0, fields, step=SHARE)
         def _(f0):
             fs = [f0 + j for j in range(SHARE)]
+
+            @pl.when(g >= 2)
+            def _():
+                copy_out(g - 2, slot, f0).wait()
+
             squares = [acc[f] for f in fs]
             for k, values in moved_chunks(turned, move_ref, fs, band, wide):
                 valid = left > k * LANES
@@ -193,44 +200,53 @@
                     squares[j] = squares[j] + mean * mean
             for j, f in enumerate(fs):
                 acc[f] = squares[j]
-
-        copy_out(g, slot).start()
+            copy_out(g, slot, f0).start()
 
     row = lax.broadcasted_iota(jnp.int32, (SUB, LANES), 0)
     total = jnp.zeros((SUB, LANES), jnp.float32)
     for f in range(fields):
-        total = jnp.where(lane == f, jnp.sum(acc[f]), total)
-    ocean = jnp.sum(jnp.where(lane[:1] == 0, count_ref[...], 0).astype(jnp.float32))
-    total = jnp.where(row == 1, ocean, total)
+        total = jnp.where(row == f, jnp.sum(acc[f], axis=0, keepdims=True), total)
+    ocean = jnp.zeros_like(lane)
+    for g in range(groups):
+        ocean = ocean + count_ref[g * SUB : (g + 1) * SUB, :]
+    ocean = jnp.where(lane == 0, ocean, 0).astype(jnp.float32)
+    total = jnp.where(row == fields, jnp.sum(ocean, axis=0, keepdims=True), total)
     for p in range(sum_ref.shape[0]):
         sum_ref[p] = total
     for g in range(groups - 2, groups):
-        copy_out(g, g % 2).wait()
+        for f0 in range(0, fields, SHARE):
+            copy_out(g, g % 2, f0).wait()
 
 
 def finish_kernel(part_ref, rms_ref):
+    fields = rms_ref.shape[1]
     total = part_ref[0]
     for p in range(1, part_ref.shape[0]):
         total = total + part_ref[p]
-    rms = jnp.sqrt(total[0:1] / total[1:2] + 1e-06)
-    rms_ref[...] = rms[:, : rms_ref.shape[1]]
+    level = jnp.sum(total, axis=1, keepdims=True)
+    rms = jnp.sqrt(level / level[fields : fields + 1] + 1e-06)
+    row = lax.broadcasted_iota(jnp.int32, (SUB, LANES), 0)
+    lane = lax.broadcasted_iota(jnp.int32, (SUB, LANES), 1)
+    flat = jnp.sum(jnp.where(row == lane, rms, 0.0), axis=0, keepdims=True)
+    rms_ref[...] = flat[:, :fields]
 
 
 VMEM = pl.BlockSpec(memory_space=pltpu.VMEM)
 
 
-def cut(fields):
+def cut(rounds, fields, grant):
     nfield, _, nrow, ncol = fields.shape
-    rounds = len(ROUNDS)
     piece = jax.ShapeDtypeStruct((nfield, nrow // 2, ncol), jnp.float32)
     return pl.pallas_call(
-        cut_kernel,
-        out_shape=(piece,) * rounds,
+        functools.partial(cut_kernel, rounds),
+        out_shape=(piece,) * len(rounds),
         in_specs=[pl.BlockSpec(memory_space=pltpu.HBM)],
-        out_specs=(VMEM,) * rounds,
-        scratch_shapes=[pltpu.SemaphoreType.DMA((rounds,))],
-        compiler_params=pltpu.CompilerParams(vmem_limit_bytes=46 << 20),
-        cost_estimate=pl.CostEstimate(flops=0, bytes_accessed=12 << 20, transcendentals=0),
+        out_specs=(VMEM,) * len(rounds),
+        scratch_shapes=[pltpu.SemaphoreType.DMA((len(rounds),))],
+        compiler_params=pltpu.CompilerParams(vmem_limit_bytes=grant << 18),
+        cost_estimate=pl.CostEstimate(
+            flops=0, bytes_accessed=800_000 * len(rounds), transcendentals=0
+        ),
         name="cut",
     )(fields)
 
@@ -285,7 +301,7 @@
         scratch_shapes=[
             pltpu.VMEM((2, fields, SUB, width), jnp.float32),
             pltpu.VMEM((fields, SUB, LANES), jnp.float32),
-            pltpu.SemaphoreType.DMA((2,)),
+            pltpu.SemaphoreType.DMA((2, fields // SHARE)),
         ],
         compiler_params=pltpu.CompilerParams(vmem_limit_bytes=6 << 20),
         cost_estimate=pl.CostEstimate(flops=40_000_000, bytes_accessed=16 << 20, transcendentals=0),
@@ -306,7 +322,9 @@
 
 def on_device(fields, mean_old, land_mask):
     nfield = fields.shape[0]
-    cuts = cut(fields)
+    cuts = []
+    for low, high, grant in zip(CUTS, CUTS[1:], GRANTS):
+        cuts += cut(ROUNDS[low:high], fields, grant)
     pieces = []
     for k, rnd in enumerate(ROUNDS):
         pieces.append(lax.ppermute(cuts[k], ("io", "cmp"), pairs_of(rnd)))

time: 147 us -> 136 us (0.925)
  waiting for transfers between devices: 6.83 us -> 51.3 us
  starting transfers between devices: 86.3 us -> 44.3 us
  blocking collectives: 28.5 us -> 13.8 us
    ppermute x16, waiting for transfers between devices: 6.83 us -> 51.3 us  [on_device(): pieces.append(lax.ppermute(cuts[k], ('io', 'cmp'), pairs_of(rnd)))]
    ppermute x16, starting transfers between devices: 86.3 us -> 44.3 us  [on_device(): pieces.append(lax.ppermute(cuts[k], ('io', 'cmp'), pairs_of(rnd)))]
    all_to_all x1, blocking collectives: 28.5 us -> 13.8 us  [on_device(): rms = finish(lax.all_to_all(part, 'io', 0, 0, tiled=True), nfield)]
    pallas_call x1 -> x2, Pallas kernels: 3.07 us -> 3.95 us  [cut(): pl.pallas_call(functools.partial(cut_kernel, rounds), out_shape=(piece,)...]
    pallas_call x3 -> x4, Pallas kernels: 4.1 us -> 4.64 us  [turn(): pl.pallas_call(functools.partial(turn_kernel, rounds, len(before)), out_s...]
  transfers between devices with their start and end apart: 16 -> 16, of which waited for: 2 -> 5; matrix products, arithmetic and copies ran while one was open for 0% -> 0% of each run, Pallas kernels for 10% -> 13%
where the time goes in v2:
time: 136 us; the launch traced here: 135 us
  waiting for transfers between devices  51.3 us (38%)
  starting transfers between devices  44.3 us (33%)
  Pallas kernels  25 us (18%)
  blocking collectives  13.8 us (10%)
    ppermute x16, waiting for transfers between devices, on_device(): pieces.append(lax.ppermute(cuts[k], ('io', 'cmp'), pairs_of(rnd)))  51.3 us
    ppermute x16, starting transfers between devices, on_device(): pieces.append(lax.ppermute(cuts[k], ('io', 'cmp'), pairs_of(rnd)))  44.3 us
    all_to_all x1, blocking collectives, on_device(): rms = finish(lax.all_to_all(part, 'io', 0, 0, tiled=True), nfield)  13.8 us
    pallas_call x1, Pallas kernels, row_indices(): pl.pallas_call(index_kernel, out_shape=(jax.ShapeDtypeStruct((rows, ncol)...  11.7 us
    pallas_call x4, Pallas kernels, turn(): pl.pallas_call(functools.partial(turn_kernel, rounds, len(before)), out_s...  4.64 us
    pallas_call x1, Pallas kernels, pack(): pl.pallas_call(pack_kernel, out_shape=(jax.ShapeDtypeStruct(old.shape, jn...  4.08 us
    pallas_call x2, Pallas kernels, cut(): pl.pallas_call(functools.partial(cut_kernel, rounds), out_shape=(piece,)...  3.95 us
  transfers between devices with their start and end apart: 16, of which 5 were waited for; matrix products, arithmetic and copies ran while one was open for 0% of the time, Pallas kernels for 13%

profile of v2, /device:TPU:0, one launch (start us, length us, event | category | flops | bytes accessed | tf_op | source)
XLA Modules:
  0.0 135.3 jit_solution(6550513187006947671)
XLA Ops:
  0.6 1.6 %cut.3 = (f32[6,64,256]{2,1,0:T(8,128)S(1)}, f32[6,64,256]{2,1,0:T(8,128)S(1)}, f32[6,64,256]{2,1,0:T(8,128)S(1)}, f32[6,64,256]{2,1,0:T(8,128)S(1)}) custom-call(f32[6,8,128,256]{3,2,1,0:T(8,128)} %fields_ref.3), custom_call_target="tpu_custom_call" | custom-call | bytes 3200000 | tf_op jit(solution)/shard_map/cut/pallas_call | solution.py:240
  2.2 2.7 %collective-permute-start.8 = (f32[6,64,256]{2,1,0:T(8,128)S(1)}, f32[6,64,256]{2,1,0:T(8,128)S(1)}, u32[]{:S(2)}, u32[]{:S(2)}) collective-permute-start(f32[6,64,256]{2,1,0:T(8,128)S(1)} %get-tuple-element.33), channel_id=1, source_target_pairs={{0,10},{1,26},{2,44},{3,60},{4,78},{5,94},{6,104},{7,120},{8,2},{9... | collective-permute-start | bytes 1179656 | tf_op jit(solution)/shard_map/ppermute | solution.py:330
  4.9 5.1 %collective-permute-start.9 = (f32[6,64,256]{2,1,0:T(8,128)S(1)}, f32[6,64,256]{2,1,0:T(8,128)S(1)}, u32[]{:S(2)}, u32[]{:S(2)}) collective-permute-start(f32[6,64,256]{2,1,0:T(8,128)S(1)} %get-tuple-element.34), channel_id=1, source_target_pairs={{0,14},{1,30},{2,40},{3,56},{4,74},{5,90},{6,108},{7,124},{8,6},{9... | collective-permute-start | bytes 1179656 | tf_op jit(solution)/shard_map/ppermute | solution.py:330
  10.0 1.3 collective-permute-start.10
  11.3 3.1 %collective-permute-start.11 = (f32[6,64,256]{2,1,0:T(8,128)S(1)}, f32[6,64,256]{2,1,0:T(8,128)S(1)}, u32[]{:S(2)}, u32[]{:S(2)}) collective-permute-start(f32[6,64,256]{2,1,0:T(8,128)S(1)} %get-tuple-element.36), channel_id=1, source_target_pairs={{0,11},{1,27},{2,45},{3,61},{4,79},{5,95},{6,105},{7,121},{8,3},{9... | collective-permute-start | bytes 1179656 | tf_op jit(solution)/shard_map/ppermute | solution.py:330
  14.4 2.4 %cut.2 = (f32[6,64,256]{2,1,0:T(8,128)S(1)}, f32[6,64,256]{2,1,0:T(8,128)S(1)}, f32[6,64,256]{2,1,0:T(8,128)S(1)}, f32[6,64,256]{2,1,0:T(8,128)S(1)}, f32[6,64,2...) custom-call(f32[6,8,128,256]{3,2,1,0:T(8,128)} %fields_ref.3), custom_call_target="tpu_custom_call" | custom-call | bytes 9600000 | tf_op jit(solution)/shard_map/cut/pallas_call | solution.py:240
  16.8 2.0 %collective-permute-start.3 = (f32[6,64,256]{2,1,0:T(8,128)S(1)}, f32[6,64,256]{2,1,0:T(8,128)S(1)}, u32[]{:S(2)}, u32[]{:S(2)}) collective-permute-start(f32[6,64,256]{2,1,0:T(8,128)S(1)} %get-tuple-element.28), channel_id=1, source_target_pairs={{0,8},{1,24},{2,42},{3,58},{4,76},{5,92},{6,110},{7,126},{8,0},{9,... | collective-permute-start | bytes 1179656 | tf_op jit(solution)/shard_map/ppermute | solution.py:330
  18.7 3.8 %collective-permute-start.4 = (f32[6,64,256]{2,1,0:T(8,128)S(1)}, f32[6,64,256]{2,1,0:T(8,128)S(1)}, u32[]{:S(2)}, u32[]{:S(2)}) collective-permute-start(f32[6,64,256]{2,1,0:T(8,128)S(1)} %get-tuple-element.29), channel_id=1, source_target_pairs={{0,12},{1,28},{2,46},{3,62},{4,72},{5,88},{6,106},{7,122},{8,4},{9... | collective-permute-start | bytes 1179656 | tf_op jit(solution)/shard_map/ppermute | solution.py:330
  22.5 4.1 %collective-permute-start.5 = (f32[6,64,256]{2,1,0:T(8,128)S(1)}, f32[6,64,256]{2,1,0:T(8,128)S(1)}, u32[]{:S(2)}, u32[]{:S(2)}) collective-permute-start(f32[6,64,256]{2,1,0:T(8,128)S(1)} %get-tuple-element.30), channel_id=1, source_target_pairs={{0,13},{1,29},{2,47},{3,63},{4,73},{5,89},{6,107},{7,123},{8,5},{9... | collective-permute-start | bytes 1179656 | tf_op jit(solution)/shard_map/ppermute | solution.py:330
  26.7 18.0 %collective-permute-done.10.refs_2_ = f32[6,64,256]{2,1,0:T(8,128)S(1)} collective-permute-done((f32[6,64,256]{2,1,0:T(8,128)S(1)}, f32[6,64,256]{2,1,0:T(8,128)S(1)}, u32[]{:S(2)}, u32[]{:S(2)}) %collective-permute-start.10) | collective-permute-done | bytes 393248 | tf_op jit(solution)/shard_map/ppermute | solution.py:330
  44.7 1.9 %collective-permute-start.12 = (f32[6,64,256]{2,1,0:T(8,128)S(1)}, f32[6,64,256]{2,1,0:T(8,128)S(1)}, u32[]{:S(2)}, u32[]{:S(2)}) collective-permute-start(f32[6,64,256]{2,1,0:T(8,128)S(1)} %get-tuple-element.37), channel_id=1, source_target_pairs={{0,2},{1,18},{2,36},{3,52},{4,70},{5,86},{6,96},{7,112},{8,10},{9,... | collective-permute-start | bytes 1179656 | tf_op jit(solution)/shard_map/ppermute | solution.py:330
  46.6 8.3 %collective-permute-start.13 = (f32[6,64,256]{2,1,0:T(8,128)S(1)}, f32[6,64,256]{2,1,0:T(8,128)S(1)}, u32[]{:S(2)}, u32[]{:S(2)}) collective-permute-start(f32[6,64,256]{2,1,0:T(8,128)S(1)} %get-tuple-element.38), channel_id=1, source_target_pairs={{0,6},{1,22},{2,32},{3,48},{4,66},{5,82},{6,100},{7,116},{8,14},{9... | collective-permute-start | bytes 1179656 | tf_op jit(solution)/shard_map/ppermute | solution.py:330
  55.3 3.3 %collective-permute-done.12.refs_4_ = f32[6,64,256]{2,1,0:T(8,128)S(1)} collective-permute-done((f32[6,64,256]{2,1,0:T(8,128)S(1)}, f32[6,64,256]{2,1,0:T(8,128)S(1)}, u32[]{:S(2)}, u32[]{:S(2)}) %collective-permute-start.12) | collective-permute-done | bytes 393248 | tf_op jit(solution)/shard_map/ppermute | solution.py:330
  59.3 5.2 %collective-permute-done.13.refs_5_ = f32[6,64,256]{2,1,0:T(8,128)S(1)} collective-permute-done((f32[6,64,256]{2,1,0:T(8,128)S(1)}, f32[6,64,256]{2,1,0:T(8,128)S(1)}, u32[]{:S(2)}, u32[]{:S(2)}) %collective-permute-start.13) | collective-permute-done | bytes 393248 | tf_op jit(solution)/shard_map/ppermute | solution.py:330
  64.4 3.2 %collective-permute-start.1 = (f32[6,64,256]{2,1,0:T(8,128)S(1)}, f32[6,64,256]{2,1,0:T(8,128)S(1)}, u32[]{:S(2)}, u32[]{:S(2)}) collective-permute-start(f32[6,64,256]{2,1,0:T(8,128)S(1)} %get-tuple-element.26), channel_id=1, source_target_pairs={{0,4},{1,20},{2,38},{3,54},{4,64},{5,80},{6,98},{7,114},{8,12},{9,... | collective-permute-start | bytes 1179656 | tf_op jit(solution)/shard_map/ppermute | solution.py:330
  67.6 2.7 %collective-permute-done.14.refs_6_ = f32[6,64,256]{2,1,0:T(8,128)S(1)} collective-permute-done((f32[6,64,256]{2,1,0:T(8,128)S(1)}, f32[6,64,256]{2,1,0:T(8,128)S(1)}, u32[]{:S(2)}, u32[]{:S(2)}) %collective-permute-start.14) | collective-permute-done | bytes 393248 | tf_op jit(solution)/shard_map/ppermute | solution.py:330
  70.4 8.0 %collective-permute-start.2 = (f32[6,64,256]{2,1,0:T(8,128)S(1)}, f32[6,64,256]{2,1,0:T(8,128)S(1)}, u32[]{:S(2)}, u32[]{:S(2)}) collective-permute-start(f32[6,64,256]{2,1,0:T(8,128)S(1)} %get-tuple-element.27), channel_id=1, source_target_pairs={{0,5},{1,21},{2,39},{3,55},{4,65},{5,81},{6,99},{7,115},{8,13},{9,... | collective-permute-start | bytes 1179656 | tf_op jit(solution)/shard_map/ppermute | solution.py:330
  78.3 22.0 %collective-permute-done.15.refs_7_ = f32[6,64,256]{2,1,0:T(8,128)S(1)} collective-permute-done((f32[6,64,256]{2,1,0:T(8,128)S(1)}, f32[6,64,256]{2,1,0:T(8,128)S(1)}, u32[]{:S(2)}, u32[]{:S(2)}) %collective-permute-start.15) | collective-permute-done | bytes 393248 | tf_op jit(solution)/shard_map/ppermute | solution.py:330
  100.4 11.7 %row_indices.1 = (s32[64,4096]{1,0:T(8,128)S(1)}, s32[5,64,4096]{2,1,0:T(8,128)S(1)}, s32[64,128]{1,0:T(8,128)S(1)}, f32[6,64,3072]{2,1,0:T(8,128)S(1)}) custom-call(s32[64,4096]{1,0:T(8,128)S(1)} %bitcast.7, f32[6,64,3072]{2,1,0:T(8,128)S(1)} %bitcast.6), custom_call_target="tpu_custom_call" | custom-call | flops 20000000 | bytes 12582912 | tf_op jit(solution)/shard_map/row_indices/pallas_call | solution.py:256
  112.1 1.8 %turn.4.refs_5_ = f32[6,32,64,128]{3,2,1,0:T(8,128)S(1)} custom-call(s32[64,4096]{1,0:T(8,128)S(1)} %get-tuple-element.24.lane_ref, f32[6,64,256]{2,1,0:T(8,128)S(1)} %collective-permute-done.8.refs_0_, f32[6,64,256]{2,1,0:T(8,128)S(1)} %collective-permute-done.9.refs_1_, f32[6,64,256]{2,1,0:T(8,128)S(1)} %collective-permute-done.10.refs_2_, ...), custom_call_target="tpu_custom_call" | custom-call | flops 8000000 | bytes 6400000 | tf_op jit(solution)/shard_map/turn/pallas_call | solution.py:277
  113.9 1.3 turn.5.refs_2_
  115.2 0.9 turn.6.refs_1_
  116.8 4.1 %pack.1 = (f32[6,64,3072]{2,1,0:T(8,128)}, f32[16,8,128]{2,1,0:T(8,128)S(1)}) custom-call(f32[6,32,64,128]{3,2,1,0:T(8,128)S(1)} %turn.7.turned, s32[5,64,4096]{2,1,0:T(8,128)S(1)} %get-tuple-element.41.move_ref, s32[64,128]{1,0:T(8,128)S(1)} %get-tuple-element.42.count_ref, f32[6,64,3072]{2,1,0:T(8,128)S(1)} %get-tuple-element.43.old_ref), custom_call_target="tpu_custom_call" | custom-call | flops 40000000 | bytes 16777216 | tf_op jit(solution)/shard_map/pack/pallas_call | solution.py:293
  120.9 13.8 %all_to_all.5.part_ref = f32[16,8,128]{2,1,0:T(8,128)S(1)} all-to-all(f32[16,8,128]{2,1,0:T(8,128)S(1)} %get-tuple-element.45), channel_id=1, replica_groups=mesh['io'=16,'cmp'=8] {'io'}, dimensions={0} | all-to-all | bytes 131072 | tf_op jit(solution)/shard_map/all_to_all | solution.py:336
  (22 shorter events, 2.3 us)
Async XLA Ops:
  0.6 99.7 %copy-start.1 = (s32[1,64,4096]{2,1,0:T(8,128)S(1)}, s32[1,64,4096]{2,1,0:T(8,128)}, u32[]{:S(2)}) copy-start(s32[1,64,4096]{2,1,0:T(8,128)} %param.5) | copy-start | bytes 3145732
  0.6 99.7 %copy-start = (f32[6,1,64,3072]{3,2,1,0:T(8,128)S(1)}, f32[6,1,64,3072]{3,2,1,0:T(8,128)}, u32[]{:S(2)}) copy-start(f32[6,1,64,3072]{3,2,1,0:T(8,128)} %param.4) | copy-start | bytes 14155780
  2.2 16.5 %collective-permute-start.8 = (f32[6,64,256]{2,1,0:T(8,128)S(1)}, f32[6,64,256]{2,1,0:T(8,128)S(1)}, u32[]{:S(2)}, u32[]{:S(2)}) collective-permute-start(f32[6,64,256]{2,1,0:T(8,128)S(1)} %get-tuple-element.33), channel_id=1, source_target_pairs={{0,10},{1,26},{2,44},{3,60},{4,78},{5,94},{6,104},{7,120},{8,2},{9... | collective-permute-start | bytes 1179656 | tf_op jit(solution)/shard_map/ppermute | solution.py:330
  4.9 17.6 %collective-permute-start.9 = (f32[6,64,256]{2,1,0:T(8,128)S(1)}, f32[6,64,256]{2,1,0:T(8,128)S(1)}, u32[]{:S(2)}, u32[]{:S(2)}) collective-permute-start(f32[6,64,256]{2,1,0:T(8,128)S(1)} %get-tuple-element.34), channel_id=1, source_target_pairs={{0,14},{1,30},{2,40},{3,56},{4,74},{5,90},{6,108},{7,124},{8,6},{9... | collective-permute-start | bytes 1179656 | tf_op jit(solution)/shard_map/ppermute | solution.py:330
  10.0 34.7 %collective-permute-start.10 = (f32[6,64,256]{2,1,0:T(8,128)S(1)}, f32[6,64,256]{2,1,0:T(8,128)S(1)}, u32[]{:S(2)}, u32[]{:S(2)}) collective-permute-start(f32[6,64,256]{2,1,0:T(8,128)S(1)} %get-tuple-element.35), channel_id=1, source_target_pairs={{0,15},{1,31},{2,41},{3,57},{4,75},{5,91},{6,109},{7,125},{8,7},{9... | collective-permute-start | bytes 1179656 | tf_op jit(solution)/shard_map/ppermute | solution.py:330
  11.3 35.4 %collective-permute-start.11 = (f32[6,64,256]{2,1,0:T(8,128)S(1)}, f32[6,64,256]{2,1,0:T(8,128)S(1)}, u32[]{:S(2)}, u32[]{:S(2)}) collective-permute-start(f32[6,64,256]{2,1,0:T(8,128)S(1)} %get-tuple-element.36), channel_id=1, source_target_pairs={{0,11},{1,27},{2,45},{3,61},{4,79},{5,95},{6,105},{7,121},{8,3},{9... | collective-permute-start | bytes 1179656 | tf_op jit(solution)/shard_map/ppermute | solution.py:330
  16.8 38.2 %collective-permute-start.3 = (f32[6,64,256]{2,1,0:T(8,128)S(1)}, f32[6,64,256]{2,1,0:T(8,128)S(1)}, u32[]{:S(2)}, u32[]{:S(2)}) collective-permute-start(f32[6,64,256]{2,1,0:T(8,128)S(1)} %get-tuple-element.28), channel_id=1, source_target_pairs={{0,8},{1,24},{2,42},{3,58},{4,76},{5,92},{6,110},{7,126},{8,0},{9,... | collective-permute-start | bytes 1179656 | tf_op jit(solution)/shard_map/ppermute | solution.py:330
  18.7 36.3 %collective-permute-start.4 = (f32[6,64,256]{2,1,0:T(8,128)S(1)}, f32[6,64,256]{2,1,0:T(8,128)S(1)}, u32[]{:S(2)}, u32[]{:S(2)}) collective-permute-start(f32[6,64,256]{2,1,0:T(8,128)S(1)} %get-tuple-element.29), channel_id=1, source_target_pairs={{0,12},{1,28},{2,46},{3,62},{4,72},{5,88},{6,106},{7,122},{8,4},{9... | collective-permute-start | bytes 1179656 | tf_op jit(solution)/shard_map/ppermute | solution.py:330
  22.5 32.6 %collective-permute-start.5 = (f32[6,64,256]{2,1,0:T(8,128)S(1)}, f32[6,64,256]{2,1,0:T(8,128)S(1)}, u32[]{:S(2)}, u32[]{:S(2)}) collective-permute-start(f32[6,64,256]{2,1,0:T(8,128)S(1)} %get-tuple-element.30), channel_id=1, source_target_pairs={{0,13},{1,29},{2,47},{3,63},{4,73},{5,89},{6,107},{7,123},{8,5},{9... | collective-permute-start | bytes 1179656 | tf_op jit(solution)/shard_map/ppermute | solution.py:330
  44.7 13.9 %collective-permute-start.12 = (f32[6,64,256]{2,1,0:T(8,128)S(1)}, f32[6,64,256]{2,1,0:T(8,128)S(1)}, u32[]{:S(2)}, u32[]{:S(2)}) collective-permute-start(f32[6,64,256]{2,1,0:T(8,128)S(1)} %get-tuple-element.37), channel_id=1, source_target_pairs={{0,2},{1,18},{2,36},{3,52},{4,70},{5,86},{6,96},{7,112},{8,10},{9,... | collective-permute-start | bytes 1179656 | tf_op jit(solution)/shard_map/ppermute | solution.py:330
  46.6 17.8 %collective-permute-start.13 = (f32[6,64,256]{2,1,0:T(8,128)S(1)}, f32[6,64,256]{2,1,0:T(8,128)S(1)}, u32[]{:S(2)}, u32[]{:S(2)}) collective-permute-start(f32[6,64,256]{2,1,0:T(8,128)S(1)} %get-tuple-element.38), channel_id=1, source_target_pairs={{0,6},{1,22},{2,32},{3,48},{4,66},{5,82},{6,100},{7,116},{8,14},{9... | collective-permute-start | bytes 1179656 | tf_op jit(solution)/shard_map/ppermute | solution.py:330
  55.0 15.4 %collective-permute-start.14 = (f32[6,64,256]{2,1,0:T(8,128)S(1)}, f32[6,64,256]{2,1,0:T(8,128)S(1)}, u32[]{:S(2)}, u32[]{:S(2)}) collective-permute-start(f32[6,64,256]{2,1,0:T(8,128)S(1)} %get-tuple-element.39), channel_id=1, source_target_pairs={{0,7},{1,23},{2,33},{3,49},{4,67},{5,83},{6,101},{7,117},{8,15},{9... | collective-permute-start | bytes 1179656 | tf_op jit(solution)/shard_map/ppermute | solution.py:330
  55.1 45.3 %collective-permute-start.15 = (f32[6,64,256]{2,1,0:T(8,128)S(1)}, f32[6,64,256]{2,1,0:T(8,128)S(1)}, u32[]{:S(2)}, u32[]{:S(2)}) collective-permute-start(f32[6,64,256]{2,1,0:T(8,128)S(1)} %get-tuple-element.40), channel_id=1, source_target_pairs={{0,3},{1,19},{2,37},{3,53},{4,71},{5,87},{6,97},{7,113},{8,11},{9,... | collective-permute-start | bytes 1179656 | tf_op jit(solution)/shard_map/ppermute | solution.py:330
  55.2 58.7 %collective-permute-start.6 = (f32[6,64,256]{2,1,0:T(8,128)S(1)}, f32[6,64,256]{2,1,0:T(8,128)S(1)}, u32[]{:S(2)}, u32[]{:S(2)}) collective-permute-start(f32[6,64,256]{2,1,0:T(8,128)S(1)} %get-tuple-element.31), channel_id=1, source_target_pairs={{0,9},{1,25},{2,43},{3,59},{4,77},{5,93},{6,111},{7,127},{8,1},{9,... | collective-permute-start | bytes 1179656 | tf_op jit(solution)/shard_map/ppermute | solution.py:330
  58.6 55.3 %collective-permute-start.7 = (f32[6,64,256]{2,1,0:T(8,128)S(1)}, f32[6,64,256]{2,1,0:T(8,128)S(1)}, u32[]{:S(2)}, u32[]{:S(2)}) collective-permute-start(f32[6,64,256]{2,1,0:T(8,128)S(1)} %get-tuple-element.32), channel_id=1, source_target_pairs={{0,0},{1,16},{2,34},{3,50},{4,68},{5,84},{6,102},{7,118},{8,8},{9,... | collective-permute-start | bytes 1179656 | tf_op jit(solution)/shard_map/ppermute | solution.py:330
  64.4 50.8 %collective-permute-start.1 = (f32[6,64,256]{2,1,0:T(8,128)S(1)}, f32[6,64,256]{2,1,0:T(8,128)S(1)}, u32[]{:S(2)}, u32[]{:S(2)}) collective-permute-start(f32[6,64,256]{2,1,0:T(8,128)S(1)} %get-tuple-element.26), channel_id=1, source_target_pairs={{0,4},{1,20},{2,38},{3,54},{4,64},{5,80},{6,98},{7,114},{8,12},{9,... | collective-permute-start | bytes 1179656 | tf_op jit(solution)/shard_map/ppermute | solution.py:330
  70.4 44.9 %collective-permute-start.2 = (f32[6,64,256]{2,1,0:T(8,128)S(1)}, f32[6,64,256]{2,1,0:T(8,128)S(1)}, u32[]{:S(2)}, u32[]{:S(2)}) collective-permute-start(f32[6,64,256]{2,1,0:T(8,128)S(1)} %get-tuple-element.27), channel_id=1, source_target_pairs={{0,5},{1,21},{2,39},{3,55},{4,65},{5,81},{6,99},{7,115},{8,13},{9,... | collective-permute-start | bytes 1179656 | tf_op jit(solution)/shard_map/ppermute | solution.py:330
  100.3 15.8 %collective-permute-start = (f32[6,64,256]{2,1,0:T(8,128)S(1)}, f32[6,64,256]{2,1,0:T(8,128)S(1)}, u32[]{:S(2)}, u32[]{:S(2)}) collective-permute-start(f32[6,64,256]{2,1,0:T(8,128)S(1)} %get-tuple-element.25), channel_id=1, source_target_pairs={{0,1},{1,17},{2,35},{3,51},{4,69},{5,85},{6,103},{7,119},{8,9},{9,... | collective-permute-start | bytes 1179656 | tf_op jit(solution)/shard_map/ppermute | solution.py:330
